TPU v7x, 16 devices: a whole 2x2x2 slice. The times are simulated.
16 devices in a mesh: tp: 2 (over z), dp: 8 (over y, x, core).
Axes of the slice: x: 2, y: 2, z: 2, core: 2. Of those that a mesh axis runs over, the one named last changes fastest.
Arguments:
- w_in: float32 [1, 1280, 8960], P(None, None, 'tp')
- w_out: float32 [1, 6400, 1280], P(None, 'tp')
- g_in: float32 [8, 1, 1280, 8960], P('dp', None, None, 'tp')
- g_out: float32 [8, 1, 6400, 1280], P('dp', None, 'tp')
- m_in: bfloat16 [1, 1280, 8960], P(None, 'dp', 'tp')
- m_out: bfloat16 [1, 6400, 1280], P(None, 'tp', 'dp')
- r_in: float32 [1, 1280], P(None, 'dp')
- c_in: float32 [1, 8960], P(None, 'tp')
- r_out: float32 [1, 6400], P(None, 'tp')
- c_out: float32 [1, 1280], P(None, 'dp')
- learn_rate: float32 [], replicated
- weight_decay: float32 [], replicated
- beta_two: float32 [], replicated
Outputs:
- output 1: float32 [1, 1280, 8960], P(None, None, 'tp')
- output 2: float32 [1, 6400, 1280], P(None, 'tp')
- output 3: bfloat16 [1, 1280, 8960], P(None, 'dp', 'tp')
- output 4: bfloat16 [1, 6400, 1280], P(None, 'tp', 'dp')
- output 5: float32 [1, 1280], P(None, 'dp')
- output 6: float32 [1, 8960], P(None, 'tp')
- output 7: float32 [1, 6400], P(None, 'tp')
- output 8: float32 [1, 1280], P(None, 'dp')
All inputs are finite; a program needn't handle non-finite values.
Results may differ from a plain program's by a relative error of at most 0.00121538.
Values sent between devices are 32-bit elements.
A program may use at most 1 GiB of HBM per device.

v0:
```python
import jax
import jax.numpy as jnp
from jax import lax
from jax.sharding import PartitionSpec as P


def local_update(weight, grad_rep, moment, row_old, col_old, learn_rate, weight_decay, beta_two, row_axis, col_axis, row_devs, col_devs):
    dp_dim = 1 if row_axis == 'dp' else 2
    grad_part = lax.psum_scatter(grad_rep[0], 'dp', scatter_dimension=dp_dim, tiled=True)
    n_rows = grad_part.shape[1] * row_devs
    n_cols = grad_part.shape[2] * col_devs
    grad_sq = grad_part * grad_part + 1e-30
    row_mean = lax.psum(jnp.sum(grad_sq, axis=2), col_axis) / n_cols
    col_mean = lax.psum(jnp.sum(grad_sq, axis=1), row_axis) / n_rows
    row_new = beta_two * row_old + (1.0 - beta_two) * row_mean
    col_new = beta_two * col_old + (1.0 - beta_two) * col_mean
    row_avg = lax.psum(jnp.sum(row_new, axis=1), row_axis) / n_rows
    second = row_new[:, :, None] * col_new[:, None, :] / row_avg[:, None, None]
    update = grad_part / jnp.sqrt(second)
    total_sq = lax.psum(jnp.sum(update * update, axis=(1, 2)), ('tp', 'dp'))
    rms_val = jnp.sqrt(total_sq / (n_rows * n_cols))
    update = update / jnp.maximum(1.0, rms_val)[:, None, None]
    mom_new = (0.9 * moment.astype(jnp.float32) + 0.1 * update).astype(jnp.bfloat16)
    width = grad_part.shape[dp_dim]
    w_block = lax.dynamic_slice_in_dim(weight, lax.axis_index('dp') * width, width, axis=dp_dim)
    w_block = w_block - learn_rate * mom_new.astype(jnp.float32) - learn_rate * weight_decay * w_block
    w_new = lax.all_gather(w_block, 'dp', axis=dp_dim, tiled=True)
    return w_new, mom_new, row_new, col_new


def solution(mesh):
    tp_devs = mesh.shape['tp']
    dp_devs = mesh.shape['dp']

    def body(w_in, w_out, g_in, g_out, m_in, m_out, r_in, c_in, r_out, c_out, learn_rate, weight_decay, beta_two):
        in_result = local_update(w_in, g_in, m_in, r_in, c_in, learn_rate, weight_decay, beta_two, 'dp', 'tp', dp_devs, tp_devs)
        out_result = local_update(w_out, g_out, m_out, r_out, c_out, learn_rate, weight_decay, beta_two, 'tp', 'dp', tp_devs, dp_devs)
        return (in_result[0], out_result[0], in_result[1], out_result[1], in_result[2], in_result[3], out_result[2], out_result[3])

    in_specs = (P(None, None, 'tp'), P(None, 'tp', None), P('dp', None, None, 'tp'), P('dp', None, 'tp', None), P(None, 'dp', 'tp'), P(None, 'tp', 'dp'), P(None, 'dp'), P(None, 'tp'), P(None, 'tp'), P(None, 'dp'), P(), P(), P())
    out_specs = (P(None, None, 'tp'), P(None, 'tp', None), P(None, 'dp', 'tp'), P(None, 'tp', 'dp'), P(None, 'dp'), P(None, 'tp'), P(None, 'tp'), P(None, 'dp'))
    return jax.shard_map(body, mesh=mesh, in_specs=in_specs, out_specs=out_specs, check_vma=False)
```

profile of v0, /device:TPU:0, one launch (start us, length us, event | category | flops | bytes accessed | tf_op | source)
XLA Modules:
  0.0 581.6 jit_solution(8958221189364230851)
XLA Ops:
  7.2 17.9 %copy.22 = f32[1,1,3200,1280]{2,3,1,0:T(8,128)} copy(f32[1,1,3200,1280]{3,2,1,0:T(8,128)} %param.16) | data formatting | bytes 32768000 | tf_op args[3]
  25.2 0.7 reduce-scatter.3.cloned.1.call-update
  27.9 3.3 constant_dynamic-slice_fusion
  31.2 2.2 copy.24
  33.5 102.5 %reduce-scatter.5.cloned.1.call-done = f32[1,3200,160]{1,2,0:T(8,128)} async-done(((f32[1,3200,1280]{1,2,0:T(8,128)}), f32[1,3200,160]{1,2,0:T(8,128)}) %reduce-scatter.5.cloned.1.call-update) | async-done | bytes 2048016 | tf_op jit(solution)/shard_map/reduce_scatter | solution.py:9
  136.0 2.0 fusion.2
  138.0 140.4 %reduce-scatter.3.cloned.1.call-done = f32[1,160,4480]{2,1,0:T(8,128)} async-done(((f32[1,1280,4480]{2,1,0:T(8,128)}), f32[1,160,4480]{2,1,0:T(8,128)}) %reduce-scatter.3.cloned.1.call-update) | async-done | bytes 2867216 | tf_op jit(solution)/shard_map/reduce_scatter | solution.py:9
  278.5 2.7 fusion
  281.2 4.9 psum.56
  286.1 0.6 fusion.6
  286.7 22.4 %all-reduce.1 = (f32[1]{0:T(128)}, f32[1,4480]{1,0:T(1,128)S(1)}, f32[1,3200]{1,0:T(1,128)S(1)}) all-reduce(f32[1]{0:T(128)} %bitcast.3, f32[1,4480]{1,0:T(1,128)S(1)} %reduce_sum.91, f32[1,3200]{1,0:T(1,128)S(1)} %reduce_sum.97), channel_id=1, replica_groups=mesh['tp'=2,'dp'=8] {'dp'}, use_global_device_ids=true, to_apply=%region_6.0 | all-reduce | flops 7681 | bytes 61448 | tf_op jit(solution)/shard_map/psum | solution.py:17
  309.8 0.6 fusion.5
  310.4 1.2 fusion.4
  311.7 5.5 all-reduce.2
  318.0 1.5 multiply_reduce_fusion
  319.6 1.3 multiply_reduce_fusion.1
  320.8 32.9 %all-reduce = (f32[1]{0:T(128)}, f32[1]{0:T(128)}) all-reduce(f32[1]{0:T(128)} %bitcast.5, f32[1]{0:T(128)} %bitcast.12), channel_id=1, replica_groups=mesh['tp'=2,'dp'=8] {'tp','dp'}, use_global_device_ids=true, to_apply=%region_8.0 | all-reduce | flops 2 | bytes 16 | tf_op jit(solution)/shard_map/psum | solution.py:20
  354.4 5.0 multiply_subtract_fusion.1
  359.5 0.0 all-gather.3.cloned.1.call-start
  360.3 5.6 multiply_subtract_fusion
  365.9 78.8 %all-gather.5.cloned.1.call-done = f32[1,3200,1280]{1,2,0:T(8,128)} async-done(((f32[1,3200,160]{1,2,0:T(8,128)}), f32[1,3200,1280]{1,2,0:T(8,128)}) %all-gather.5.cloned.1.call-update) | async-done | bytes 16384016 | tf_op jit(solution)/shard_map/all_gather | solution.py:27
  444.7 17.9 %copy.23 = f32[1,3200,1280]{2,1,0:T(8,128)} copy(f32[1,3200,1280]{1,2,0:T(8,128)} %all-gather.5.cloned.1.call-done) | data formatting | bytes 32768000
  462.6 96.4 %all-gather.3.cloned.1.call-done = f32[1,1280,4480]{2,1,0:T(8,128)} async-done(((f32[1,160,4480]{2,1,0:T(8,128)}), f32[1,1280,4480]{2,1,0:T(8,128)}) %all-gather.3.cloned.1.call-update) | async-done | bytes 22937616 | tf_op jit(solution)/shard_map/all_gather | solution.py:27
  559.0 16.0 %copy.29 = f32[1,1280,4480]{2,1,0:T(8,128)} copy(f32[1,1280,4480]{2,1,0:T(8,128)} %all-gather.3.cloned.1.call-done) | data formatting | bytes 45875200
  (25 shorter events, 0.2 us)
Async XLA Ops:
  7.2 128.8 %reduce-scatter.5.cloned.1.call-start = ((), (), s32[]{:S(2)}) async-start(), calls=%async_computation.4 | async-start | bytes 18432000 | tf_op jit(solution)/shard_map/reduce_scatter | solution.py:9
  25.2 253.3 %reduce-scatter.3.cloned.1.call-start = ((), (), s32[]{:S(2)}) async-start(), calls=%async_computation.2 | async-start | bytes 25804800 | tf_op jit(solution)/shard_map/reduce_scatter | solution.py:9
  25.9 418.8 %all-gather.5.cloned.1.call-start = ((), (), s32[]{:S(2)}) async-start(), calls=%async_computation.5 | async-start | bytes 18432000 | tf_op jit(solution)/shard_map/all_gather | solution.py:27
  33.5 252.6 %copy-start.6 = (f32[1,160]{1,0:T(1,128)S(1)}, f32[1,160]{1,0:T(1,128)}, u32[]{:S(2)}) copy-start(f32[1,160]{1,0:T(1,128)} %param.19) | copy-start | bytes 1924
  33.5 276.3 %copy-start.2 = (f32[1,4480]{1,0:T(1,128)S(1)}, f32[1,4480]{1,0:T(1,128)}, u32[]{:S(2)}) copy-start(f32[1,4480]{1,0:T(1,128)} %param.20) | copy-start | bytes 53764
  33.5 277.0 %copy-start.3 = (f32[1,3200]{1,0:T(1,128)S(1)}, f32[1,3200]{1,0:T(1,128)}, u32[]{:S(2)}) copy-start(f32[1,3200]{1,0:T(1,128)} %param.21) | copy-start | bytes 38404
  33.5 284.5 %copy-start.7 = (f32[1,160]{1,0:T(1,128)S(1)}, f32[1,160]{1,0:T(1,128)}, u32[]{:S(2)}) copy-start(f32[1,160]{1,0:T(1,128)} %param.22) | copy-start | bytes 1924
  278.5 39.6 %copy-start = (f32[1,160,4480]{2,1,0:T(8,128)S(1)}, f32[1,160,4480]{2,1,0:T(8,128)}, u32[]{:S(2)}) copy-start(f32[1,160,4480]{2,1,0:T(8,128)} %reduce-scatter.3.cloned.1.call-done) | copy-start | bytes 8601604
  286.7 73.6 %copy-start.4 = (f32[1,160]{1,0:T(1,128)}, f32[1,160]{1,0:T(1,128)S(1)}, u32[]{:S(2)}) copy-start(f32[1,160]{1,0:T(1,128)S(1)} %get-tuple-element.50) | copy-start | bytes 1924
  317.2 2.4 copy-start.1
  318.0 41.4 %copy-start.5 = (f32[1,160]{1,0:T(1,128)}, f32[1,160]{1,0:T(1,128)S(1)}, u32[]{:S(2)}) copy-start(f32[1,160]{1,0:T(1,128)S(1)} %multiply_add_fusion.4) | copy-start | bytes 1924
  359.5 199.5 %all-gather.3.cloned.1.call-start = ((), (), s32[]{:S(2)}) async-start(), calls=%async_computation.3 | async-start | bytes 25804800 | tf_op jit(solution)/shard_map/all_gather | solution.py:27
Sparse Core Ops, SparseCore 0:
  25.3 110.6 reduce-scatter.4
  139.5 138.8 reduce-scatter.2
  359.6 85.0 all-gather.4
  447.0 111.9 all-gather.2
where the time goes:
time: 583 us; the launch traced here: 582 us
  waiting for transfers between devices  419 us (72%)
  blocking collectives  65.8 us (11%)
  local copies, waits for them, and re-layouts  57.5 us (10%)
  other arithmetic  20.6 us (4%)
  between operations  18.7 us (3%)
    reduce_scatter x2, waiting for transfers between devices, local_update(): lax.psum_scatter(grad_rep[0], 'dp', scatter_dimension=dp_dim, tiled=True)  243 us
    all_gather x2, waiting for transfers between devices, local_update(): w_new = lax.all_gather(w_block, 'dp', axis=dp_dim, tiled=True)  175 us
    unnamed x20, local copies, waits for them, and re-layouts  54.2 us
    psum x1, blocking collectives, local_update(): total_sq = lax.psum(jnp.sum(update * update, axis=(1, 2)), ('tp', 'dp'))  32.9 us
    psum x2, blocking collectives, local_update(): row_avg = lax.psum(jnp.sum(row_new, axis=1), row_axis) / n_rows  28 us
  transfers between devices with their start and end apart: 4, of which 4 were waited for; matrix products, arithmetic and copies ran while one was open for 5% of the time, Pallas kernels for 0%

commit v1 on v0

v1 whole, which is shorter than its diff:
```python
import functools

import jax
import jax.numpy as jnp
from jax import lax
from jax.experimental import pallas as pl
from jax.experimental.pallas import tpu as pltpu
from jax.sharding import PartitionSpec as P

F32 = jnp.float32
BF16 = jnp.bfloat16
MESH = pl.DeviceIdType.MESH
LANE, SUB, SUB2, PART, QUAD, WIDTH = 128, 8, 16, 32, 4, 160
NO = None

D = 1280
ROWS_IN, COLS_IN = WIDTH, 4480
ROWS_OUT, COLS_OUT = 800, 640
RAW_OUT = 3200
STEPS = 10
M_IN = ROWS_IN // STEPS // 2
M_OUT = ROWS_OUT // STEPS // 2
RAW_STEP = RAW_OUT // STEPS
TILES_OUT = RAW_OUT // LANE

GRANT = 24 << 20

N_RED = 11
N_GAT = 18
(OWN, DSS, DSR, A1S, A1R, B1S, B1R, A2S, A2R, B2S, B2R) = range(N_RED)
(OXS, OXR, OYS, OYR, OPS, OPR, FXS, FXR, FYS, FYR, PXS, PXR, PYS, PYR, PDS, PDR, _U0, _U1) = range(N_GAT)


def lanes(shape):
    return lax.broadcasted_iota(jnp.int32, shape, 1)


def aligned(value, by):
    return pl.multiple_of(value, by)


def pad_lanes(row):
    return jnp.concatenate([row, jnp.zeros((1, LANE - row.shape[1]), F32)], axis=1)


def row_to_col(row):
    return jnp.broadcast_to(row, (LANE, LANE)).T


def main_kernel(n_tp, n_dp, rows_all_in, cols_all_in, rows_all_out, cols_all_out,
                w_in, w_out, g_in, g_out, m_in, m_out, r_in, c_in, r_out, c_out, lr_ref, wd_ref, b2_ref,
                win, wpk, m_in_new, m_out_new, r_in_new, c_in_new, r_out_new, c_out_new,
                own_in, raw, packed, gs_in, gs_out, w_cols, ai_out, ai_in, bj_in, vec_x, vec_y,
                col_acc, row_acc, row_peer, col_acc_out, col_peer_out, sv_in, sv_out,
                tot1_in, tot2_in, tot1_out, tot2_out,
                red_sem, gat_sem, load_sem, sv_send, sv_recv, zv_sem, tot_send, tot_recv):
    tp = lax.axis_index('tp')
    q = lax.axis_index('dp')
    me = tp * n_dp + q
    p, c = q // 2, q % 2
    y, x = p // 2, p % 2
    p_x, p_y, p_d = 2 * y + (1 - x), 2 * (1 - y) + x, 2 * (1 - y) + (1 - x)
    to_x = {'dp': 2 * p_x + c}
    to_y = {'dp': 2 * p_y + c}
    to_core = {'dp': 2 * p + (1 - c)}
    to_z = {'tp': 1 - tp}
    n_all = n_tp * n_dp
    j = q % QUAD
    lr, wd, b2 = lr_ref[0], wd_ref[0], b2_ref[0]

    barrier = pltpu.get_barrier_semaphore()

    def greet(d, _):
        other = lax.rem(me + d, n_all)
        pl.semaphore_signal(barrier, inc=1, device_id={'tp': other // n_dp, 'dp': lax.rem(other, n_dp)}, device_id_type=MESH)
        return 0

    lax.fori_loop(1, n_all, greet, 0)
    pl.semaphore_wait(barrier, n_all - 1)

    def rcopy(src, dst, send, recv, dev):
        return pltpu.make_async_remote_copy(src_ref=src, dst_ref=dst, send_sem=send, recv_sem=recv, device_id=dev, device_id_type=MESH)

    def spans(m, t):
        base = aligned(2 * m * t, SUB)
        return pl.ds(base, 2 * m), pl.ds(base, m), pl.ds(aligned(base + m, SUB), m)

    def first_copies(ph, w, m, t):
        _, ra, rb = spans(m, t)
        a = rcopy(w.at[pl.ds(0, 2), 1 - x, ra], w.at[2, pl.ds(0, 2), ra], red_sem.at[ph, A1S, t], red_sem.at[ph, A1R, t], to_x)
        b = rcopy(w.at[1 - y, pl.ds(0, 2), rb], w.at[2, pl.ds(0, 2), rb], red_sem.at[ph, B1S, t], red_sem.at[ph, B1R, t], to_y)
        return a, b

    def second_copies(ph, w, m, t):
        _, ra, rb = spans(m, t)
        a = rcopy(w.at[1 - y, x, ra], w.at[3, 0, ra], red_sem.at[ph, A2S, t], red_sem.at[ph, A2R, t], to_y)
        b = rcopy(w.at[y, 1 - x, rb], w.at[3, 0, rb], red_sem.at[ph, B2S, t], red_sem.at[ph, B2R, t], to_x)
        return a, b

    def pair_in(t):
        rr, _, _ = spans(M_IN, t)
        return rcopy(g_in.at[:, :, 1 - c, rr], win.at[pl.ds(0, 2), :, rr], red_sem.at[0, DSS, t], red_sem.at[0, DSR, t], to_core)

    def own_load(t):
        rr, _, _ = spans(M_IN, t)
        return pltpu.make_async_copy(g_in.at[:, :, c, rr], own_in.at[lax.rem(t, 3)], red_sem.at[0, OWN, t])

    def raw_load(t):
        return pltpu.make_async_copy(g_out.at[pl.ds(aligned(RAW_STEP * t, SUB), RAW_STEP)], raw.at[lax.rem(t, 2)], red_sem.at[1, OWN, t])

    def pair_out(t):
        rr, _, _ = spans(M_OUT, t)
        return rcopy(packed.at[lax.rem(t, 2), :, :, 1 - c], wpk.at[pl.ds(0, 2), :, rr], red_sem.at[1, DSS, t], red_sem.at[1, DSR, t], to_core)

    def start_in(t):
        pair_in(t).start()
        own_load(t).start()

    def pack_out(t):
        raw_load(t).wait()
        slot = lax.rem(t, 2)

        @pl.when(t >= 2)
        def _():
            pair_out(t - 2).wait_send()

        def unit(u, _):
            base = aligned(PART * u, SUB)
            tiles = [[raw[slot, pl.ds(base + SUB * k, SUB), LANE * i:LANE * i + LANE] for i in range(10)] for k in range(QUAD)]
            ln = lanes((SUB, LANE))
            for s in range(SUB):
                jj, first = s % QUAD, 5 * (s // QUAD) + s % QUAD
                tail = NO
                for k in range(QUAD):
                    lo, hi = tiles[k][first], tiles[k][first + 1]
                    head = lo if jj == 0 else pltpu.roll(jnp.where(ln >= PART * jj, lo, hi), LANE - PART * jj, 1)
                    packed[slot, s // QUAD, (s // 2) % 2, s % 2, pl.ds(aligned(SUB * u, SUB), SUB), LANE * k:LANE * k + LANE] = head
                    turn = (PART * (k - jj)) % LANE
                    part = hi if turn == 0 else pltpu.roll(hi, turn, 1)
                    tail = part if tail is NO else jnp.where(ln >= PART * k, part, tail)
                packed[slot, s // QUAD, (s // 2) % 2, s % 2, pl.ds(aligned(SUB * u, SUB), SUB), 512:640] = tail
            return 0

        lax.fori_loop(0, RAW_STEP // PART, unit, 0)
        pair_out(t).start()

        @pl.when(t + 2 < STEPS)
        def _():
            raw_load(t + 2).start()

    def reduce_first(ph, w, m, t):
        rr, _, _ = spans(m, t)
        if ph == 0:
            own_load(t).wait()
            pair_in(t).wait_recv()
            slot = lax.rem(t, 3)
            for yy in range(2):
                for xx in range(2):
                    for r in range(0, 2 * m, SUB):
                        rows = pl.ds(aligned(2 * m * t + r, SUB), SUB)
                        w[yy, xx, rows] = w[yy, xx, rows] + own_in[slot, yy, xx, r:r + SUB]
        else:
            pair_out(t).wait_recv()
            slot = lax.rem(t, 2)

            def add(i, _):
                rows = pl.ds(aligned(2 * m * t + SUB2 * i, SUB), SUB2)
                for yy in range(2):
                    for xx in range(2):
                        w[yy, xx, rows] = w[yy, xx, rows] + packed[slot, yy, xx, c, pl.ds(aligned(SUB2 * i, SUB), SUB2)]
                return 0

            lax.fori_loop(0, 2 * m // SUB2, add, 0)
        for copy in first_copies(ph, w, m, t):
            copy.start()

    def reduce_second(ph, w, m, t):
        _, ra, rb = spans(m, t)
        a, b = first_copies(ph, w, m, t)
        a2, b2_ = second_copies(ph, w, m, t)
        a.wait_recv()
        w[1 - y, x, ra] = w[1 - y, x, ra] + w[2, 1 - y, ra]
        a2.start()
        b.wait_recv()
        w[y, 1 - x, rb] = w[y, 1 - x, rb] + w[2, 1 - x, rb]
        b2_.start()

    def reduce_third(ph, w, m, t, gs):
        _, ra, rb = spans(m, t)
        first, second = first_copies(ph, w, m, t), second_copies(ph, w, m, t)
        second[0].wait_recv()
        ga = w[y, x, ra] + w[2, y, ra] + w[3, 0, ra]
        gs[ra] = ga
        second[1].wait_recv()
        gb = w[y, x, rb] + w[2, x, rb] + w[3, 0, rb]
        gs[rb] = gb
        for copy in (*first, *second):
            copy.wait_send()
        if ph == 0:
            pair_in(t).wait_send()
            sa, sb = ga * ga + 1e-30, gb * gb + 1e-30
            col_acc[...] = col_acc[...] + (sa + sb)
            for rows, sq in ((ra, sa), (rb, sb)):
                part = sq[:, 0:LANE]
                for i in range(1, COLS_IN // LANE):
                    part = part + sq[:, LANE * i:LANE * i + LANE]
                row_acc[rows] = part

    def gather_own(ph, w, m, t):
        rr, _, _ = spans(m, t)
        src = w.at[p, c, rr]
        return (rcopy(src, src, gat_sem.at[ph, OXS, t], gat_sem.at[ph, OXR, t], to_x),
                rcopy(src, src, gat_sem.at[ph, OYS, t], gat_sem.at[ph, OYR, t], to_y),
                rcopy(src, src, gat_sem.at[ph, OPS, t], gat_sem.at[ph, OPR, t], to_core))

    def gather_came(ph, w, m, t):
        rr, _, _ = spans(m, t)
        return (rcopy(w.at[p_x, c, rr], w.at[p_x, c, rr], gat_sem.at[ph, OXS, t], gat_sem.at[ph, OXR, t], to_x),
                rcopy(w.at[p_y, c, rr], w.at[p_y, c, rr], gat_sem.at[ph, OYS, t], gat_sem.at[ph, OYR, t], to_y))

    def gather_on(ph, w, m, t):
        _, ra, rb = spans(m, t)
        return (rcopy(w.at[p_y, c, ra], w.at[p_y, c, ra], gat_sem.at[ph, FXS, t], gat_sem.at[ph, FXR, t], to_x),
                rcopy(w.at[p_x, c, rb], w.at[p_x, c, rb], gat_sem.at[ph, FYS, t], gat_sem.at[ph, FYR, t], to_y))

    def gather_diag(ph, w, m, t):
        _, ra, rb = spans(m, t)
        return (rcopy(w.at[p_d, c, ra], w.at[p_d, c, ra], gat_sem.at[ph, FXS, t], gat_sem.at[ph, FXR, t], to_x),
                rcopy(w.at[p_d, c, rb], w.at[p_d, c, rb], gat_sem.at[ph, FYS, t], gat_sem.at[ph, FYR, t], to_y))

    def gather_pair(ph, w, m, t, cc):
        rr, _, _ = spans(m, t)
        return [rcopy(w.at[pp, cc, rr], w.at[pp, cc, rr], gat_sem.at[ph, s, t], gat_sem.at[ph, s + 1, t], to_core)
                for pp, s in ((p_x, PXS), (p_y, PYS), (p_d, PDS))]

    def gather_first(ph, w, m, t):
        for copy in gather_own(ph, w, m, t):
            copy.start()

    def gather_second(ph, w, m, t):
        came = gather_came(ph, w, m, t)
        on = gather_on(ph, w, m, t)
        pair = gather_pair(ph, w, m, t, c)
        came[0].wait_recv()
        on[1].start()
        pair[0].start()
        came[1].wait_recv()
        on[0].start()
        pair[1].start()

    def gather_third(ph, w, m, t):
        diag = gather_diag(ph, w, m, t)
        diag[0].wait_recv()
        diag[1].wait_recv()
        gather_pair(ph, w, m, t, c)[2].start()

    def gather_last(ph, w, m, t):
        rr, _, _ = spans(m, t)
        own_pair = rcopy(w.at[p, 1 - c, rr], w.at[p, 1 - c, rr], gat_sem.at[ph, OPS, t], gat_sem.at[ph, OPR, t], to_core)
        own_pair.wait_recv()
        for copy in gather_pair(ph, w, m, t, 1 - c):
            copy.wait_recv()
        for copy in (*gather_own(ph, w, m, t), *gather_on(ph, w, m, t), *gather_pair(ph, w, m, t, c)):
            copy.wait_send()

    def to_all(buf, which):
        def send(d, _):
            other = lax.rem(me + d, n_all)
            dev = {'tp': other // n_dp, 'dp': lax.rem(other, n_dp)}
            rcopy(buf.at[me], buf.at[me], tot_send.at[which, d], tot_recv.at[which, me], dev).start()
            return 0

        lax.fori_loop(1, n_all, send, 0)

    def from_all(buf, which):
        def take(d, _):
            other = lax.rem(me + d, n_all)
            rcopy(buf.at[other], buf.at[other], tot_send.at[which, d], tot_recv.at[which, other], to_z).wait()
            return 0

        lax.fori_loop(1, n_all, take, 0)

    def to_group(buf, which):
        def send(d, _):
            other = lax.rem(q + d, n_dp)
            rcopy(buf.at[q], buf.at[q], sv_send.at[which, d], sv_recv.at[which, q], {'dp': other}).start()
            return 0

        lax.fori_loop(1, n_dp, send, 0)

    def from_group(buf, which):
        def take(d, _):
            other = lax.rem(q + d, n_dp)
            rcopy(buf.at[other], buf.at[other], sv_send.at[which, d], sv_recv.at[which, other], to_z).wait()
            return 0

        lax.fori_loop(1, n_dp, take, 0)

    def add_all(buf, n):
        total = buf[0]
        for i in range(1, n):
            total = total + buf[i]
        return total

    def z_in():
        return rcopy(row_acc, row_peer, zv_sem.at[0], zv_sem.at[1], to_z)

    def z_out():
        return rcopy(col_acc_out, col_peer_out, zv_sem.at[2], zv_sem.at[3], to_z)

    def total(value):
        return jnp.sum(jnp.sum(value, axis=0, keepdims=True), axis=1, keepdims=True)

    def old_total(ref, width):
        acc = jnp.zeros((1, LANE), F32)
        for i in range(0, width, LANE):
            part = ref[:, i:min(i + LANE, width)]
            acc = acc + (part if part.shape[1] == LANE else pad_lanes(part))
        return jnp.broadcast_to(total(acc), (SUB, LANE))

    def stats_in_send():
        part = col_acc[:, 0:LANE]
        for i in range(1, COLS_IN // LANE):
            part = part + col_acc[:, LANE * i:LANE * i + LANE]
        sv_in[q] = jnp.sum(col_acc[...], axis=0, keepdims=True)
        tot1_in[me, 0:SUB] = part
        tot1_in[me, SUB:SUB2] = old_total(r_in, ROWS_IN)
        z_in().start()
        to_group(sv_in, 0)
        to_all(tot1_in, 0)
        w_load_in().start()

    def w_load_in():
        return pltpu.make_async_copy(w_in.at[p, c], win.at[p, c], load_sem.at[0])

    def stats_in_norm():
        z_in().wait()
        from_group(sv_in, 0)
        from_all(tot1_in, 0)
        col_mean = add_all(sv_in, n_dp) / rows_all_in
        c_new = b2 * c_in[...] + (1.0 - b2) * col_mean
        c_in_new[...] = c_new
        bj_in[...] = 1.0 / jnp.sqrt(c_new)
        all_tot = add_all(tot1_in, n_all)
        r_total = all_tot[SUB:9, 0:1] / n_tp
        r_avg = (b2 * r_total + (1.0 - b2) * (total(all_tot[0:SUB]) / cols_all_in)) / rows_all_in
        root_avg = jnp.sqrt(r_avg)
        row_mean = jnp.sum(row_acc[...] + row_peer[...], axis=1, keepdims=True) / cols_all_in
        row_mean = jnp.broadcast_to(row_mean, (ROWS_IN, LANE))
        r_old = jnp.concatenate([row_to_col(r_in[:, 0:LANE]), row_to_col(pad_lanes(r_in[:, LANE:WIDTH]))[0:PART]], axis=0)
        r_new = b2 * r_old + (1.0 - b2) * row_mean
        r_in_new[:, 0:LANE] = r_new[0:LANE].T[0:1]
        r_in_new[:, LANE:WIDTH] = jnp.concatenate([r_new[LANE:WIDTH], jnp.zeros((96, LANE), F32)], axis=0).T[0:1, 0:PART]
        ai_in[...] = root_avg / jnp.sqrt(r_new)

        def body(i, acc):
            rows = pl.ds(aligned(SUB * i, SUB), SUB)
            a = ai_in[rows]
            for k in range(COLS_IN // LANE):
                col = slice(LANE * k, LANE * k + LANE)
                u = gs_in[rows, col] * a * bj_in[:, col]
                acc = acc + u * u
            return acc

        tot2_in[me] = lax.fori_loop(0, ROWS_IN // SUB, body, jnp.zeros((SUB, LANE), F32))
        to_all(tot2_in, 1)

    def scale_of(buf, count):
        mean = total(add_all(buf, n_all)) / count
        return 0.1 / jnp.maximum(1.0, jnp.sqrt(mean))

    def update_in():
        from_all(tot2_in, 1)
        scale = scale_of(tot2_in, float(rows_all_in * cols_all_in))
        w_load_in().wait()
        m_load_in().wait()

        def body(i, _):
            rows = pl.ds(aligned(SUB2 * i, SUB2), SUB2)
            a = ai_in[rows] * scale
            for k in range(COLS_IN // LANE):
                col = slice(LANE * k, LANE * k + LANE)
                u = gs_in[rows, col] * a * bj_in[:, col]
                mom = (0.9 * m_in_new[rows, col].astype(F32) + u).astype(BF16)
                m_in_new[rows, col] = mom
                old = win[p, c, rows, col]
                win[p, c, rows, col] = old - lr * mom.astype(F32) - lr * wd * old
            return 0

        lax.fori_loop(0, ROWS_IN // SUB2, body, 0)

    def m_load_in():
        return pltpu.make_async_copy(m_in, m_in_new, load_sem.at[1])

    def block_out(t):
        heads, tails = [], []
        for u in range(QUAD):
            rows = pl.ds(aligned(PART * t + SUB * u, SUB), SUB)
            tail = gs_out[rows, 512:640]
            for k in range(QUAD):
                heads.append(gs_out[rows, LANE * k:LANE * k + LANE])
                tails.append(tail if k == 0 else pltpu.roll(tail, LANE - PART * k, 1))
        tails = jnp.concatenate(tails, axis=0)
        return jnp.concatenate(heads, axis=0), jnp.where(lanes((LANE, LANE)) < PART, tails, 0.0)

    def stats_out_send():
        def body(t, acc):
            head, tail = block_out(t)
            sh = head * head + 1e-30
            st = jnp.where(lanes((LANE, LANE)) < PART, tail * tail + 1e-30, 0.0)
            sv_out[q, :, pl.ds(aligned(LANE * t, LANE), LANE)] = jnp.sum((sh + st).T, axis=0, keepdims=True)
            ah, at = acc
            for i in range(SUB2):
                ah = ah + sh[SUB * i:SUB * i + SUB]
                at = at + st[SUB * i:SUB * i + SUB]
            return ah, at

        zero = jnp.zeros((SUB, LANE), F32)
        ah, at = lax.fori_loop(0, TILES_OUT, body, (zero, zero))
        col_acc_out[0:SUB] = ah
        col_acc_out[SUB:SUB2] = at
        tot1_out[me, 0:SUB] = ah + at
        tot1_out[me, SUB:SUB2] = old_total(r_out, RAW_OUT)
        z_out().start()
        to_group(sv_out, 1)
        to_all(tot1_out, 2)

    def stats_out_norm():
        z_out().wait()
        from_group(sv_out, 1)
        from_all(tot1_out, 2)
        row_mean = add_all(sv_out, n_dp) / cols_all_out
        r_new = b2 * r_out[...] + (1.0 - b2) * row_mean
        r_out_new[...] = r_new
        all_tot = add_all(tot1_out, n_all)
        r_total = all_tot[SUB:9, 0:1] / n_dp
        r_avg = (b2 * r_total + (1.0 - b2) * (total(all_tot[0:SUB]) / cols_all_out)) / rows_all_out
        root_avg = jnp.sqrt(r_avg)
        cols = col_acc_out[...] + col_peer_out[...]
        c_new_h = b2 * c_out[:, 0:LANE] + (1.0 - b2) * (jnp.sum(cols[0:SUB], axis=0, keepdims=True) / rows_all_out)
        c_new_t = b2 * pad_lanes(c_out[:, LANE:WIDTH]) + (1.0 - b2) * (jnp.sum(cols[SUB:SUB2], axis=0, keepdims=True) / rows_all_out)
        c_out_new[:, 0:LANE] = c_new_h
        c_out_new[:, LANE:WIDTH] = c_new_t[:, 0:PART]
        vec_x[...] = jnp.broadcast_to(1.0 / jnp.sqrt(c_new_h), (SUB, LANE))
        vec_y[...] = jnp.broadcast_to(1.0 / jnp.sqrt(jnp.where(lanes((1, LANE)) < PART, c_new_t, 1.0)), (SUB, LANE))
        bh, bt = vec_x[0:1], vec_y[0:1]

        def body(t, acc):
            rows = pl.ds(aligned(LANE * t, LANE), LANE)
            a = row_to_col(root_avg / jnp.sqrt(r_out_new[:, rows]))
            ai_out[rows] = a
            head, tail = block_out(t)
            uh, ut = head * a * bh, tail * a * bt
            sq = uh * uh + ut * ut
            for i in range(SUB2):
                acc = acc + sq[SUB * i:SUB * i + SUB]
            return acc

        tot2_out[me] = lax.fori_loop(0, TILES_OUT, body, jnp.zeros((SUB, LANE), F32))
        to_all(tot2_out, 3)

    def w_load_out():
        first = 5 * (q // QUAD) + j
        return pltpu.make_async_copy(w_out.at[:, pl.ds(aligned(LANE * first, LANE), 256)], w_cols, load_sem.at[2])

    def m_load_out():
        return pltpu.make_async_copy(m_out, m_out_new, load_sem.at[3])

    def update_out():
        from_all(tot2_out, 3)
        scale = scale_of(tot2_out, float(rows_all_out * cols_all_out))
        w_load_out().wait()
        m_load_out().wait()
        bh, bt = vec_x[0:1], vec_y[0:1]
        back = PART * ((QUAD - j) % QUAD)

        def body(t, _):
            rows = pl.ds(aligned(LANE * t, LANE), LANE)
            a = ai_out[rows] * scale
            head, tail = block_out(t)
            uh, ut = head * a * bh, tail * a * bt
            mom = m_out_new[:, rows].astype(F32)
            mh = (0.9 * mom[0:LANE].T + uh).astype(BF16).astype(F32)
            mt = (0.9 * jnp.concatenate([mom[LANE:WIDTH], jnp.zeros((96, LANE), F32)], axis=0).T + ut).astype(BF16).astype(F32)
            m_out_new[0:LANE, rows] = mh.T.astype(BF16)
            m_out_new[LANE:WIDTH, rows] = mt.T[0:PART].astype(BF16)
            lo, hi = w_cols[rows, 0:LANE], w_cols[rows, LANE:256]
            wh = pltpu.roll(jnp.where(lanes((LANE, LANE)) >= PART * j, lo, hi), back, 1)
            wt = pltpu.roll(hi, back, 1)
            wh = wh - lr * mh - lr * wd * wh
            wt = wt - lr * mt - lr * wd * wt
            ln = lanes((SUB, LANE))
            for u in range(QUAD):
                to = pl.ds(aligned(PART * t + SUB * u, SUB), SUB)
                joined = NO
                for k in range(QUAD):
                    at = PART * u + SUB * k
                    wpk[p, c, to, LANE * k:LANE * k + LANE] = wh[at:at + SUB]
                    part = wt[at:at + SUB] if k == 0 else pltpu.roll(wt[at:at + SUB], PART * k, 1)
                    joined = part if joined is NO else jnp.where(ln >= PART * k, part, joined)
                wpk[p, c, to, 512:640] = joined
            return 0

        lax.fori_loop(0, TILES_OUT, body, 0)

    col_acc[...] = jnp.zeros_like(col_acc)
    start_in(0)
    start_in(1)

    def at_step(cond, fn, *args):
        @pl.when(cond)
        def _():
            fn(*args)

    n = STEPS

    def step(s, _):
        def within(lo, hi):
            return jnp.logical_and(s >= lo, s < hi)

        at_step(s + 2 < n, start_in, s + 2)
        at_step(s < n, reduce_first, 0, win, M_IN, s)
        at_step(within(2, n + 2), reduce_second, 0, win, M_IN, s - 2)
        at_step(within(QUAD, n + QUAD), reduce_third, 0, win, M_IN, s - QUAD, gs_in)

        @pl.when(s == 2)
        def _():
            m_load_in().start()
            m_load_out().start()
            w_load_out().start()

        @pl.when(s == n - 3)
        def _():
            raw_load(0).start()
            raw_load(1).start()

        at_step(within(n, 2 * n), reduce_first, 1, wpk, M_OUT, s - n)
        at_step(within(n - 1, 2 * n - 1), pack_out, s - n + 1)
        at_step(within(n + 2, 2 * n + 2), reduce_second, 1, wpk, M_OUT, s - n - 2)
        at_step(within(n + QUAD, 2 * n + QUAD), reduce_third, 1, wpk, M_OUT, s - n - QUAD, gs_out)
        at_step(s == n + 3, stats_in_send)
        at_step(s == n + 6, stats_in_norm)
        at_step(s == n + 9, update_in)
        at_step(within(2 * n, 3 * n), gather_first, 0, win, M_IN, s - 2 * n)
        at_step(within(2 * n + 2, 3 * n + 2), gather_second, 0, win, M_IN, s - 2 * n - 2)
        at_step(within(2 * n + QUAD, 3 * n + QUAD), gather_third, 0, win, M_IN, s - 2 * n - QUAD)
        at_step(s == 2 * n + 3, stats_out_send)
        at_step(s == 2 * n + 6, stats_out_norm)
        at_step(s == 2 * n + 9, update_out)
        at_step(within(3 * n, QUAD * n), gather_first, 1, wpk, M_OUT, s - 3 * n)
        at_step(within(3 * n + 2, QUAD * n + 2), gather_second, 1, wpk, M_OUT, s - 3 * n - 2)
        at_step(within(3 * n + QUAD, QUAD * n + QUAD), gather_third, 1, wpk, M_OUT, s - 3 * n - QUAD)
        return 0

    lax.fori_loop(0, QUAD * n + QUAD, step, 0)

    def finish(t, _):
        gather_last(0, win, M_IN, t)
        gather_last(1, wpk, M_OUT, t)
        return 0

    lax.fori_loop(0, n, finish, 0)
    pair_out(n - 2).wait_send()
    pair_out(n - 1).wait_send()


def final_kernel(win, wpk, mi, mo, ri, ci, ro, co, win_o, wout_o, mi_o, mo_o, ri_o, ci_o, ro_o, co_o, stage, sem, stage_sem):
    plain = [pltpu.make_async_copy(win, win_o, sem.at[0])]
    for i, (src, dst) in enumerate(((mi, mi_o), (mo, mo_o), (ri, ri_o), (ci, ci_o), (ro, ro_o), (co, co_o))):
        plain.append(pltpu.make_async_copy(src, dst, sem.at[i + 1]))
    for copy in plain:
        copy.start()

    def rows_of(t):
        return pl.ds(aligned(RAW_STEP * t, SUB), RAW_STEP)

    def put(t):
        return pltpu.make_async_copy(stage.at[rows_of(t)], wout_o.at[rows_of(t)], stage_sem.at[t])

    def chunk(t, _):
        def unit(u, _):
            ln = lanes((SUB, LANE))
            rows = pl.ds(aligned(2 * M_OUT * t + SUB * u, SUB), SUB)
            for half in range(2):
                tails = [wpk[2 * half + jj // 2, jj % 2, rows, 512:640] for jj in range(QUAD)]
                for k in range(QUAD):
                    to = pl.ds(aligned(RAW_STEP * t + PART * u + SUB * k, SUB), SUB)
                    heads = []
                    for jj in range(QUAD):
                        head = wpk[2 * half + jj // 2, jj % 2, rows, LANE * k:LANE * k + LANE]
                        heads.append(head if jj == 0 else pltpu.roll(head, PART * jj, 1))
                    ends = [tails[jj] if jj == k else pltpu.roll(tails[jj], (PART * (jj - k)) % LANE, 1) for jj in range(QUAD)]
                    for tile in range(5):
                        if tile == 0:
                            out = heads[0]
                        else:
                            out = ends[tile - 1]
                            if tile > 1:
                                out = jnp.where(ln < PART * (tile - 1), heads[tile - 1], out)
                            if tile < QUAD:
                                out = jnp.where(ln >= PART * tile, heads[tile], out)
                        at = LANE * (5 * half + tile)
                        stage[to, at:at + LANE] = out
            return 0

        lax.fori_loop(0, RAW_STEP // PART, unit, 0)
        put(t).start()
        return 0

    lax.fori_loop(0, STEPS, chunk, 0)
    for t in range(STEPS):
        put(t).wait()
    for copy in plain:
        copy.wait()


def solution(mesh):
    n_tp = mesh.shape['tp']
    n_dp = mesh.shape['dp']
    vmem = pl.BlockSpec(memory_space=pltpu.VMEM)
    hbm = pl.BlockSpec(memory_space=pltpu.HBM)
    smem = pl.BlockSpec(memory_space=pltpu.SMEM)
    dma = pltpu.SemaphoreType.DMA
    kept = (
        ((QUAD, 2, ROWS_IN, COLS_IN), F32),
        ((QUAD, 2, ROWS_OUT, COLS_OUT), F32),
        ((ROWS_IN, COLS_IN), BF16),
        ((WIDTH, RAW_OUT), BF16),
        ((1, ROWS_IN), F32),
        ((1, COLS_IN), F32),
        ((1, RAW_OUT), F32),
        ((1, WIDTH), F32),
    )
    main = pl.pallas_call(
        functools.partial(main_kernel, n_tp, n_dp, D, COLS_IN * n_tp, RAW_OUT * n_tp, D),
        out_shape=[pltpu.VMEM(shape, dtype) for shape, dtype in kept],
        in_specs=[hbm] * 6 + [vmem] * QUAD + [smem] * 3,
        out_specs=[vmem] * SUB,
        scratch_shapes=[
            pltpu.VMEM((3, 2, 2, 2 * M_IN, COLS_IN), F32),
            pltpu.VMEM((2, RAW_STEP, D), F32),
            pltpu.VMEM((2, 2, 2, 2, 2 * M_OUT, COLS_OUT), F32),
            pltpu.VMEM((ROWS_IN, COLS_IN), F32),
            pltpu.VMEM((ROWS_OUT, COLS_OUT), F32),
            pltpu.VMEM((RAW_OUT, 256), F32),
            pltpu.VMEM((RAW_OUT, LANE), F32),
            pltpu.VMEM((ROWS_IN, LANE), F32),
            pltpu.VMEM((1, COLS_IN), F32),
            pltpu.VMEM((SUB, LANE), F32),
            pltpu.VMEM((SUB, LANE), F32),
            pltpu.VMEM((SUB, COLS_IN), F32),
            pltpu.VMEM((ROWS_IN, LANE), F32),
            pltpu.VMEM((ROWS_IN, LANE), F32),
            pltpu.VMEM((SUB2, LANE), F32),
            pltpu.VMEM((SUB2, LANE), F32),
            pltpu.VMEM((n_dp, 1, COLS_IN), F32),
            pltpu.VMEM((n_dp, 1, RAW_OUT), F32),
            pltpu.VMEM((n_tp * n_dp, SUB2, LANE), F32),
            pltpu.VMEM((n_tp * n_dp, SUB, LANE), F32),
            pltpu.VMEM((n_tp * n_dp, SUB2, LANE), F32),
            pltpu.VMEM((n_tp * n_dp, SUB, LANE), F32),
            dma((2, N_RED, STEPS)),
            dma((2, N_GAT, STEPS)),
            dma((QUAD,)),
            dma((2, n_dp)),
            dma((2, n_dp)),
            dma((QUAD,)),
            dma((QUAD, n_tp * n_dp)),
            dma((QUAD, n_tp * n_dp)),
        ],
        compiler_params=pltpu.CompilerParams(collective_id=0, has_side_effects=True, vmem_limit_bytes=GRANT),
    )
    final = pl.pallas_call(
        final_kernel,
        out_shape=[
            jax.ShapeDtypeStruct((QUAD, 2, ROWS_IN, COLS_IN), F32),
            jax.ShapeDtypeStruct((RAW_OUT, D), F32),
        ] + [jax.ShapeDtypeStruct(shape, dtype) for shape, dtype in kept[2:]],
        in_specs=[vmem] * SUB,
        out_specs=[hbm] * SUB,
        scratch_shapes=[pltpu.VMEM((RAW_OUT, D), F32), dma((7,)), dma((STEPS,))],
        compiler_params=pltpu.CompilerParams(vmem_limit_bytes=GRANT),
    )

    def body(w_in, w_out, g_in, g_out, m_in, m_out, r_in, c_in, r_out, c_out, learn_rate, weight_decay, beta_two):
        shards = (QUAD, 2, ROWS_IN, COLS_IN)
        got = main(
            w_in.reshape(shards), w_out[0], g_in.reshape((2, 2, 2, ROWS_IN, COLS_IN)), g_out[0, 0], m_in[0], m_out[0].T,
            r_in, c_in, r_out, c_out, learn_rate.reshape(1), weight_decay.reshape(1), beta_two.reshape(1))
        w_i, w_o, m_i, m_o, r_i, c_i, r_o, c_o = final(*[pltpu.with_memory_space_constraint(g, pltpu.VMEM) for g in got])
        return w_i.reshape((1, D, COLS_IN)), w_o[NO], m_i[NO], m_o.T[NO], r_i, c_i, r_o, c_o

    in_specs = (P(NO, NO, 'tp'), P(NO, 'tp', NO), P('dp', NO, NO, 'tp'), P('dp', NO, 'tp', NO), P(NO, 'dp', 'tp'), P(NO, 'tp', 'dp'), P(NO, 'dp'), P(NO, 'tp'), P(NO, 'tp'), P(NO, 'dp'), P(), P(), P())
    out_specs = (P(NO, NO, 'tp'), P(NO, 'tp', NO), P(NO, 'dp', 'tp'), P(NO, 'tp', 'dp'), P(NO, 'dp'), P(NO, 'tp'), P(NO, 'tp'), P(NO, 'dp'))
    return jax.shard_map(body, mesh=mesh, in_specs=in_specs, out_specs=out_specs, check_vma=False)
```

time: 583 us -> 358 us (0.61)
  waiting for transfers between devices: 419 us -> 0 us
  Pallas kernels: 0 us -> 355 us
  blocking collectives: 65.8 us -> 0 us
  local copies, waits for them, and re-layouts: 57.5 us -> 0 us
  other arithmetic: 20.6 us -> 0 us
  between operations: 18.7 us -> 2.58 us
    pallas_call x0 -> x2, Pallas kernels: none -> 355 us  [the longest x1 341 us: body(): main(w_in.reshape(shards), w_out[0], g_in.reshape((2, 2, 2, ROWS_IN, COLS...]
    reduce_scatter x2 -> x0, waiting for transfers between devices: 243 us -> none  [local_update(): lax.psum_scatter(grad_rep[0], 'dp', scatter_dimension=dp_dim, tiled=True)]
    all_gather x2 -> x0, waiting for transfers between devices: 175 us -> none  [local_update(): w_new = lax.all_gather(w_block, 'dp', axis=dp_dim, tiled=True)]
    psum x4 -> x0, blocking collectives: 65.8 us -> none  [the longest x1 32.9 us: local_update(): total_sq = lax.psum(jnp.sum(update * update, axis=(1, 2)), ('tp', 'dp'))]
    unnamed x20 -> x0, local copies, waits for them, and re-layouts: 54.2 us -> none
    sub x2 -> x0, other arithmetic: 10.6 us -> none  [local_update(): w_block - learn_rate * mom_new.astype(jnp.float32)]
    reduce_sum x5 -> x0, other arithmetic: 8.13 us -> none  [the longest x2 4.74 us: local_update(): col_mean = lax.psum(jnp.sum(grad_sq, axis=1), row_axis) / n_rows]
  transfers between devices with their start and end apart: 4 -> 0, of which waited for: 4 -> 0; matrix products, arithmetic and copies ran while one was open for 5% -> 0% of each run, Pallas kernels for 0% -> 0%
where the time goes in v1:
time: 358 us
  Pallas kernels  355 us (99%)
    pallas_call x1, Pallas kernels, body(): main(w_in.reshape(shards), w_out[0], g_in.reshape((2, 2, 2, ROWS_IN, COLS...  341 us
    pallas_call x1, Pallas kernels, body(): final(*[pltpu.with_memory_space_constraint(g, pltpu.VMEM) for g in got])  14.1 us

profile of v1, /device:TPU:0, one launch (start us, length us, event | category | flops | bytes accessed | tf_op | source)
XLA Modules:
  0.0 357.6 jit_solution(16627741686142198751)
XLA Ops:
  2.6 340.9 %shard_map.188 = (f32[4,2,160,4480]{3,2,1,0:T(8,128)S(1)}, f32[4,2,800,640]{3,2,1,0:T(8,128)S(1)}, bf16[160,4480]{1,0:T(8,128)(2,1)S(1)}, bf16[160,3200]{1,0:T(8...) custom-call(f32[4,2,160,4480]{3,2,1,0:T(8,128)} %bitcast.20, ...), custom_call_target="tpu_custom_call" | custom-call | tf_op jit(solution)/shard_map/pallas_call | solution.py:687
  343.5 14.1 %shard_map.189 = (f32[4,2,160,4480]{3,2,1,0:T(8,128)}, f32[3200,1280]{1,0:T(8,128)}, bf16[160,4480]{1,0:T(8,128)(2,1)}, bf16[160,3200]{1,0:T(8,128)(2,1)}, f32[1...) custom-call(f32[4,2,160,4480]{3,2,1,0:T(8,128)S(1)} %get-tuple-element.24.win, ...), custom_call_target="tpu_custom_call" | custom-call | tf_op jit(solution)/shard_map/pallas_call | solution.py:690

commit v2 on v1

--- a/solution.py
+++ b/solution.py
@@ -26,9 +26,10 @@
 GRANT = 24 << 20
 
 N_RED = 11
-N_GAT = 18
+N_GAT = 16
+SLOTS = 6
 (OWN, DSS, DSR, A1S, A1R, B1S, B1R, A2S, A2R, B2S, B2R) = range(N_RED)
-(OXS, OXR, OYS, OYR, OPS, OPR, FXS, FXR, FYS, FYR, PXS, PXR, PYS, PYR, PDS, PDR, _U0, _U1) = range(N_GAT)
+(OXS, OXR, OYS, OYR, OPS, OPR, FXS, FXR, FYS, FYR, PXS, PXR, PYS, PYR, PDS, PDR) = range(N_GAT)
 
 
 def lanes(shape):
@@ -51,35 +52,31 @@
                 w_in, w_out, g_in, g_out, m_in, m_out, r_in, c_in, r_out, c_out, lr_ref, wd_ref, b2_ref,
                 win, wpk, m_in_new, m_out_new, r_in_new, c_in_new, r_out_new, c_out_new,
                 own_in, raw, packed, gs_in, gs_out, w_cols, ai_out, ai_in, bj_in, vec_x, vec_y,
-                col_acc, row_acc, row_peer, col_acc_out, col_peer_out, sv_in, sv_out,
-                tot1_in, tot2_in, tot1_out, tot2_out,
-                red_sem, gat_sem, load_sem, sv_send, sv_recv, zv_sem, tot_send, tot_recv):
+                col_acc, row_acc, row_peer, col_acc_out, col_peer_out, v_in, vc_in, v_out, vc_out,
+                zt_in, pt_in, ct_in, zt_out, pt_out, ct_out,
+                red_sem, gat_sem, load_sem, ex_sem):
     tp = lax.axis_index('tp')
     q = lax.axis_index('dp')
-    me = tp * n_dp + q
     p, c = q // 2, q % 2
     y, x = p // 2, p % 2
     p_x, p_y, p_d = 2 * y + (1 - x), 2 * (1 - y) + x, 2 * (1 - y) + (1 - x)
     to_x = {'dp': 2 * p_x + c}
     to_y = {'dp': 2 * p_y + c}
+    to_d = {'dp': 2 * p_d + c}
     to_core = {'dp': 2 * p + (1 - c)}
     to_z = {'tp': 1 - tp}
-    n_all = n_tp * n_dp
     j = q % QUAD
     lr, wd, b2 = lr_ref[0], wd_ref[0], b2_ref[0]
 
     barrier = pltpu.get_barrier_semaphore()
-
-    def greet(d, _):
-        other = lax.rem(me + d, n_all)
-        pl.semaphore_signal(barrier, inc=1, device_id={'tp': other // n_dp, 'dp': lax.rem(other, n_dp)}, device_id_type=MESH)
-        return 0
-
-    lax.fori_loop(1, n_all, greet, 0)
-    pl.semaphore_wait(barrier, n_all - 1)
+    for dev in (to_x, to_y, to_core, to_z):
+        pl.semaphore_signal(barrier, inc=1, device_id=dev, device_id_type=MESH)
 
     def rcopy(src, dst, send, recv, dev):
         return pltpu.make_async_remote_copy(src_ref=src, dst_ref=dst, send_sem=send, recv_sem=recv, device_id=dev, device_id_type=MESH)
+
+    def slot_of(ph, t):
+        return lax.rem(ph * STEPS + t, SLOTS)
 
     def spans(m, t):
         base = aligned(2 * m * t, SUB)
@@ -87,34 +84,34 @@
 
     def first_copies(ph, w, m, t):
         _, ra, rb = spans(m, t)
-        a = rcopy(w.at[pl.ds(0, 2), 1 - x, ra], w.at[2, pl.ds(0, 2), ra], red_sem.at[ph, A1S, t], red_sem.at[ph, A1R, t], to_x)
-        b = rcopy(w.at[1 - y, pl.ds(0, 2), rb], w.at[2, pl.ds(0, 2), rb], red_sem.at[ph, B1S, t], red_sem.at[ph, B1R, t], to_y)
+        a = rcopy(w.at[pl.ds(0, 2), 1 - x, ra], w.at[2, pl.ds(0, 2), ra], red_sem.at[A1S, slot_of(ph, t)], red_sem.at[A1R, slot_of(ph, t)], to_x)
+        b = rcopy(w.at[1 - y, pl.ds(0, 2), rb], w.at[2, pl.ds(0, 2), rb], red_sem.at[B1S, slot_of(ph, t)], red_sem.at[B1R, slot_of(ph, t)], to_y)
         return a, b
 
     def second_copies(ph, w, m, t):
         _, ra, rb = spans(m, t)
-        a = rcopy(w.at[1 - y, x, ra], w.at[3, 0, ra], red_sem.at[ph, A2S, t], red_sem.at[ph, A2R, t], to_y)
-        b = rcopy(w.at[y, 1 - x, rb], w.at[3, 0, rb], red_sem.at[ph, B2S, t], red_sem.at[ph, B2R, t], to_x)
+        a = rcopy(w.at[1 - y, x, ra], w.at[3, 0, ra], red_sem.at[A2S, slot_of(ph, t)], red_sem.at[A2R, slot_of(ph, t)], to_y)
+        b = rcopy(w.at[y, 1 - x, rb], w.at[3, 0, rb], red_sem.at[B2S, slot_of(ph, t)], red_sem.at[B2R, slot_of(ph, t)], to_x)
         return a, b
 
     def pair_in(t):
         rr, _, _ = spans(M_IN, t)
-        return rcopy(g_in.at[:, :, 1 - c, rr], win.at[pl.ds(0, 2), :, rr], red_sem.at[0, DSS, t], red_sem.at[0, DSR, t], to_core)
+        return rcopy(g_in.at[:, :, 1 - c, rr], win.at[pl.ds(0, 2), :, rr], red_sem.at[DSS, slot_of(0, t)], red_sem.at[DSR, slot_of(0, t)], to_core)
 
     def own_load(t):
         rr, _, _ = spans(M_IN, t)
-        return pltpu.make_async_copy(g_in.at[:, :, c, rr], own_in.at[lax.rem(t, 3)], red_sem.at[0, OWN, t])
+        return pltpu.make_async_copy(g_in.at[:, :, c, rr], own_in.at[lax.rem(t, 3)], red_sem.at[OWN, slot_of(0, t)])
 
     def raw_load(t):
-        return pltpu.make_async_copy(g_out.at[pl.ds(aligned(RAW_STEP * t, SUB), RAW_STEP)], raw.at[lax.rem(t, 2)], red_sem.at[1, OWN, t])
+        return pltpu.make_async_copy(g_out.at[pl.ds(aligned(RAW_STEP * t, SUB), RAW_STEP)], raw.at[lax.rem(t, 2)], red_sem.at[OWN, slot_of(1, t)])
 
     def pair_out(t):
         rr, _, _ = spans(M_OUT, t)
-        return rcopy(packed.at[lax.rem(t, 2), :, :, 1 - c], wpk.at[pl.ds(0, 2), :, rr], red_sem.at[1, DSS, t], red_sem.at[1, DSR, t], to_core)
+        return rcopy(packed.at[lax.rem(t, 2), :, :, 1 - c], wpk.at[pl.ds(0, 2), :, rr], red_sem.at[DSS, slot_of(1, t)], red_sem.at[DSR, slot_of(1, t)], to_core)
 
     def start_in(t):
+        own_load(t).start()
         pair_in(t).start()
-        own_load(t).start()
 
     def pack_out(t):
         raw_load(t).wait()
@@ -178,6 +175,8 @@
         _, ra, rb = spans(m, t)
         a, b = first_copies(ph, w, m, t)
         a2, b2_ = second_copies(ph, w, m, t)
+        if ph == 0:
+            pair_in(t).wait_send()
         a.wait_recv()
         w[1 - y, x, ra] = w[1 - y, x, ra] + w[2, 1 - y, ra]
         a2.start()
@@ -197,7 +196,6 @@
         for copy in (*first, *second):
             copy.wait_send()
         if ph == 0:
-            pair_in(t).wait_send()
             sa, sb = ga * ga + 1e-30, gb * gb + 1e-30
             col_acc[...] = col_acc[...] + (sa + sb)
             for rows, sq in ((ra, sa), (rb, sb)):
@@ -209,28 +207,28 @@
     def gather_own(ph, w, m, t):
         rr, _, _ = spans(m, t)
         src = w.at[p, c, rr]
-        return (rcopy(src, src, gat_sem.at[ph, OXS, t], gat_sem.at[ph, OXR, t], to_x),
-                rcopy(src, src, gat_sem.at[ph, OYS, t], gat_sem.at[ph, OYR, t], to_y),
-                rcopy(src, src, gat_sem.at[ph, OPS, t], gat_sem.at[ph, OPR, t], to_core))
+        return (rcopy(src, src, gat_sem.at[OXS, slot_of(ph, t)], gat_sem.at[OXR, slot_of(ph, t)], to_x),
+                rcopy(src, src, gat_sem.at[OYS, slot_of(ph, t)], gat_sem.at[OYR, slot_of(ph, t)], to_y),
+                rcopy(src, src, gat_sem.at[OPS, slot_of(ph, t)], gat_sem.at[OPR, slot_of(ph, t)], to_core))
 
     def gather_came(ph, w, m, t):
         rr, _, _ = spans(m, t)
-        return (rcopy(w.at[p_x, c, rr], w.at[p_x, c, rr], gat_sem.at[ph, OXS, t], gat_sem.at[ph, OXR, t], to_x),
-                rcopy(w.at[p_y, c, rr], w.at[p_y, c, rr], gat_sem.at[ph, OYS, t], gat_sem.at[ph, OYR, t], to_y))
+        return (rcopy(w.at[p_x, c, rr], w.at[p_x, c, rr], gat_sem.at[OXS, slot_of(ph, t)], gat_sem.at[OXR, slot_of(ph, t)], to_x),
+                rcopy(w.at[p_y, c, rr], w.at[p_y, c, rr], gat_sem.at[OYS, slot_of(ph, t)], gat_sem.at[OYR, slot_of(ph, t)], to_y))
 
     def gather_on(ph, w, m, t):
         _, ra, rb = spans(m, t)
-        return (rcopy(w.at[p_y, c, ra], w.at[p_y, c, ra], gat_sem.at[ph, FXS, t], gat_sem.at[ph, FXR, t], to_x),
-                rcopy(w.at[p_x, c, rb], w.at[p_x, c, rb], gat_sem.at[ph, FYS, t], gat_sem.at[ph, FYR, t], to_y))
+        return (rcopy(w.at[p_y, c, ra], w.at[p_y, c, ra], gat_sem.at[FXS, slot_of(ph, t)], gat_sem.at[FXR, slot_of(ph, t)], to_x),
+                rcopy(w.at[p_x, c, rb], w.at[p_x, c, rb], gat_sem.at[FYS, slot_of(ph, t)], gat_sem.at[FYR, slot_of(ph, t)], to_y))
 
     def gather_diag(ph, w, m, t):
         _, ra, rb = spans(m, t)
-        return (rcopy(w.at[p_d, c, ra], w.at[p_d, c, ra], gat_sem.at[ph, FXS, t], gat_sem.at[ph, FXR, t], to_x),
-                rcopy(w.at[p_d, c, rb], w.at[p_d, c, rb], gat_sem.at[ph, FYS, t], gat_sem.at[ph, FYR, t], to_y))
+        return (rcopy(w.at[p_d, c, ra], w.at[p_d, c, ra], gat_sem.at[FXS, slot_of(ph, t)], gat_sem.at[FXR, slot_of(ph, t)], to_x),
+                rcopy(w.at[p_d, c, rb], w.at[p_d, c, rb], gat_sem.at[FYS, slot_of(ph, t)], gat_sem.at[FYR, slot_of(ph, t)], to_y))
 
     def gather_pair(ph, w, m, t, cc):
         rr, _, _ = spans(m, t)
-        return [rcopy(w.at[pp, cc, rr], w.at[pp, cc, rr], gat_sem.at[ph, s, t], gat_sem.at[ph, s + 1, t], to_core)
+        return [rcopy(w.at[pp, cc, rr], w.at[pp, cc, rr], gat_sem.at[s, slot_of(ph, t)], gat_sem.at[s + 1, slot_of(ph, t)], to_core)
                 for pp, s in ((p_x, PXS), (p_y, PYS), (p_d, PDS))]
 
     def gather_first(ph, w, m, t):
@@ -238,6 +236,7 @@
             copy.start()
 
     def gather_second(ph, w, m, t):
+        rr, _, _ = spans(m, t)
         came = gather_came(ph, w, m, t)
         on = gather_on(ph, w, m, t)
         pair = gather_pair(ph, w, m, t, c)
@@ -247,103 +246,83 @@
         came[1].wait_recv()
         on[0].start()
         pair[1].start()
+        rcopy(w.at[p, 1 - c, rr], w.at[p, 1 - c, rr], gat_sem.at[OPS, slot_of(ph, t)], gat_sem.at[OPR, slot_of(ph, t)], to_core).wait_recv()
 
     def gather_third(ph, w, m, t):
         diag = gather_diag(ph, w, m, t)
         diag[0].wait_recv()
         diag[1].wait_recv()
         gather_pair(ph, w, m, t, c)[2].start()
+        for copy in gather_pair(ph, w, m, t, 1 - c)[:2]:
+            copy.wait_recv()
+        for copy in gather_own(ph, w, m, t):
+            copy.wait_send()
 
     def gather_last(ph, w, m, t):
-        rr, _, _ = spans(m, t)
-        own_pair = rcopy(w.at[p, 1 - c, rr], w.at[p, 1 - c, rr], gat_sem.at[ph, OPS, t], gat_sem.at[ph, OPR, t], to_core)
-        own_pair.wait_recv()
-        for copy in gather_pair(ph, w, m, t, 1 - c):
-            copy.wait_recv()
-        for copy in (*gather_own(ph, w, m, t), *gather_on(ph, w, m, t), *gather_pair(ph, w, m, t, c)):
+        gather_pair(ph, w, m, t, 1 - c)[2].wait_recv()
+        for copy in (*gather_on(ph, w, m, t), *gather_pair(ph, w, m, t, c)):
             copy.wait_send()
 
-    def to_all(buf, which):
-        def send(d, _):
-            other = lax.rem(me + d, n_all)
-            dev = {'tp': other // n_dp, 'dp': lax.rem(other, n_dp)}
-            rcopy(buf.at[me], buf.at[me], tot_send.at[which, d], tot_recv.at[which, me], dev).start()
-            return 0
-
-        lax.fori_loop(1, n_all, send, 0)
-
-    def from_all(buf, which):
-        def take(d, _):
-            other = lax.rem(me + d, n_all)
-            rcopy(buf.at[other], buf.at[other], tot_send.at[which, d], tot_recv.at[which, other], to_z).wait()
-            return 0
-
-        lax.fori_loop(1, n_all, take, 0)
-
-    def to_group(buf, which):
-        def send(d, _):
-            other = lax.rem(q + d, n_dp)
-            rcopy(buf.at[q], buf.at[q], sv_send.at[which, d], sv_recv.at[which, q], {'dp': other}).start()
-            return 0
-
-        lax.fori_loop(1, n_dp, send, 0)
-
-    def from_group(buf, which):
-        def take(d, _):
-            other = lax.rem(q + d, n_dp)
-            rcopy(buf.at[other], buf.at[other], sv_send.at[which, d], sv_recv.at[which, other], to_z).wait()
-            return 0
-
-        lax.fori_loop(1, n_dp, take, 0)
-
-    def add_all(buf, n):
-        total = buf[0]
-        for i in range(1, n):
-            total = total + buf[i]
-        return total
-
-    def z_in():
-        return rcopy(row_acc, row_peer, zv_sem.at[0], zv_sem.at[1], to_z)
-
-    def z_out():
-        return rcopy(col_acc_out, col_peer_out, zv_sem.at[2], zv_sem.at[3], to_z)
-
-    def total(value):
-        return jnp.sum(jnp.sum(value, axis=0, keepdims=True), axis=1, keepdims=True)
-
-    def old_total(ref, width):
+    def z_share(src, dst, k):
+        return rcopy(src, dst, ex_sem.at[k, 0], ex_sem.at[k, 1], to_z)
+
+    def share(buf, k):
+        copy = rcopy(buf.at[0], buf.at[1], ex_sem.at[k, 2], ex_sem.at[k, 3], to_core)
+        copy.start()
+        copy.wait()
+        return buf[0] + buf[1]
+
+    def to_chips(buf, k):
+        for i, dev in enumerate((to_x, to_y, to_d)):
+            rcopy(buf.at[p], buf.at[p], ex_sem.at[k, QUAD + i], ex_sem.at[k, QUAD + 3 + i], dev).start()
+
+    def from_chips(buf, k):
+        for i, (dev, other) in enumerate(((to_x, p_x), (to_y, p_y), (to_d, p_d))):
+            rcopy(buf.at[other], buf.at[other], ex_sem.at[k, QUAD + i], ex_sem.at[k, QUAD + 3 + i], dev).wait()
+        return buf[0] + buf[1] + buf[2] + buf[3]
+
+    def old_lanes(ref, width):
         acc = jnp.zeros((1, LANE), F32)
         for i in range(0, width, LANE):
             part = ref[:, i:min(i + LANE, width)]
             acc = acc + (part if part.shape[1] == LANE else pad_lanes(part))
-        return jnp.broadcast_to(total(acc), (SUB, LANE))
+        return acc
+
+    def share_squares(acc, zt, pt, ct):
+        zt[0] = jnp.sum(acc, axis=0, keepdims=True)
+        copy = z_share(zt.at[0], zt.at[1], 1)
+        copy.start()
+        copy.wait()
+        pt[0] = zt[0] + zt[1]
+        ct[p] = share(pt, 1)
+        to_chips(ct, 1)
+
+    def scale_from(ct, count):
+        mean = jnp.sum(from_chips(ct, 1), axis=1, keepdims=True) / count
+        return 0.1 / jnp.maximum(1.0, jnp.sqrt(mean))
 
     def stats_in_send():
-        part = col_acc[:, 0:LANE]
-        for i in range(1, COLS_IN // LANE):
-            part = part + col_acc[:, LANE * i:LANE * i + LANE]
-        sv_in[q] = jnp.sum(col_acc[...], axis=0, keepdims=True)
-        tot1_in[me, 0:SUB] = part
-        tot1_in[me, SUB:SUB2] = old_total(r_in, ROWS_IN)
-        z_in().start()
-        to_group(sv_in, 0)
-        to_all(tot1_in, 0)
+        copy = z_share(row_acc, row_peer, 0)
+        copy.start()
+        v_in[0, :, 0:COLS_IN] = jnp.sum(col_acc[...], axis=0, keepdims=True)
+        v_in[0, :, COLS_IN + LANE:COLS_IN + 2 * LANE] = old_lanes(r_in, ROWS_IN)
+        copy.wait()
+        v_in[0, :, COLS_IN:COLS_IN + LANE] = jnp.sum(row_acc[...] + row_peer[...], axis=0, keepdims=True)
+        vc_in[p] = share(v_in, 0)
+        to_chips(vc_in, 0)
         w_load_in().start()
 
     def w_load_in():
         return pltpu.make_async_copy(w_in.at[p, c], win.at[p, c], load_sem.at[0])
 
     def stats_in_norm():
-        z_in().wait()
-        from_group(sv_in, 0)
-        from_all(tot1_in, 0)
-        col_mean = add_all(sv_in, n_dp) / rows_all_in
-        c_new = b2 * c_in[...] + (1.0 - b2) * col_mean
+        vec = from_chips(vc_in, 0)
+        c_new = b2 * c_in[...] + (1.0 - b2) * (vec[:, 0:COLS_IN] / rows_all_in)
         c_in_new[...] = c_new
         bj_in[...] = 1.0 / jnp.sqrt(c_new)
-        all_tot = add_all(tot1_in, n_all)
-        r_total = all_tot[SUB:9, 0:1] / n_tp
-        r_avg = (b2 * r_total + (1.0 - b2) * (total(all_tot[0:SUB]) / cols_all_in)) / rows_all_in
+        s_total = jnp.sum(vec[:, COLS_IN:COLS_IN + LANE], axis=1, keepdims=True)
+        r_total = jnp.sum(vec[:, COLS_IN + LANE:COLS_IN + 2 * LANE], axis=1, keepdims=True)
+        r_avg = (b2 * r_total + (1.0 - b2) * (s_total / cols_all_in)) / rows_all_in
         root_avg = jnp.sqrt(r_avg)
         row_mean = jnp.sum(row_acc[...] + row_peer[...], axis=1, keepdims=True) / cols_all_in
         row_mean = jnp.broadcast_to(row_mean, (ROWS_IN, LANE))
@@ -362,16 +341,10 @@
                 acc = acc + u * u
             return acc
 
-        tot2_in[me] = lax.fori_loop(0, ROWS_IN // SUB, body, jnp.zeros((SUB, LANE), F32))
-        to_all(tot2_in, 1)
-
-    def scale_of(buf, count):
-        mean = total(add_all(buf, n_all)) / count
-        return 0.1 / jnp.maximum(1.0, jnp.sqrt(mean))
+        share_squares(lax.fori_loop(0, ROWS_IN // SUB, body, jnp.zeros((SUB, LANE), F32)), zt_in, pt_in, ct_in)
 
     def update_in():
-        from_all(tot2_in, 1)
-        scale = scale_of(tot2_in, float(rows_all_in * cols_all_in))
+        scale = scale_from(ct_in, float(rows_all_in * cols_all_in))
         w_load_in().wait()
         m_load_in().wait()
 
@@ -408,7 +381,7 @@
             head, tail = block_out(t)
             sh = head * head + 1e-30
             st = jnp.where(lanes((LANE, LANE)) < PART, tail * tail + 1e-30, 0.0)
-            sv_out[q, :, pl.ds(aligned(LANE * t, LANE), LANE)] = jnp.sum((sh + st).T, axis=0, keepdims=True)
+            v_out[0, :, pl.ds(aligned(LANE * t, LANE), LANE)] = jnp.sum((sh + st).T, axis=0, keepdims=True)
             ah, at = acc
             for i in range(SUB2):
                 ah = ah + sh[SUB * i:SUB * i + SUB]
@@ -419,22 +392,20 @@
         ah, at = lax.fori_loop(0, TILES_OUT, body, (zero, zero))
         col_acc_out[0:SUB] = ah
         col_acc_out[SUB:SUB2] = at
-        tot1_out[me, 0:SUB] = ah + at
-        tot1_out[me, SUB:SUB2] = old_total(r_out, RAW_OUT)
-        z_out().start()
-        to_group(sv_out, 1)
-        to_all(tot1_out, 2)
+        col_acc_out[SUB2:SUB2 + SUB] = jnp.broadcast_to(old_lanes(r_out, RAW_OUT), (SUB, LANE))
+        copy = z_share(col_acc_out, col_peer_out, 0)
+        copy.start()
+        copy.wait()
+        v_out[0, :, RAW_OUT:RAW_OUT + LANE] = jnp.sum(col_acc_out[0:SUB2] + col_peer_out[0:SUB2], axis=0, keepdims=True)
+        vc_out[p] = share(v_out, 0)
+        to_chips(vc_out, 0)
 
     def stats_out_norm():
-        z_out().wait()
-        from_group(sv_out, 1)
-        from_all(tot1_out, 2)
-        row_mean = add_all(sv_out, n_dp) / cols_all_out
-        r_new = b2 * r_out[...] + (1.0 - b2) * row_mean
-        r_out_new[...] = r_new
-        all_tot = add_all(tot1_out, n_all)
-        r_total = all_tot[SUB:9, 0:1] / n_dp
-        r_avg = (b2 * r_total + (1.0 - b2) * (total(all_tot[0:SUB]) / cols_all_out)) / rows_all_out
+        vec = from_chips(vc_out, 0)
+        r_out_new[...] = b2 * r_out[...] + (1.0 - b2) * (vec[:, 0:RAW_OUT] / cols_all_out)
+        s_total = jnp.sum(vec[:, RAW_OUT:RAW_OUT + LANE], axis=1, keepdims=True)
+        r_total = jnp.sum((col_acc_out[SUB2:SUB2 + SUB] + col_peer_out[SUB2:SUB2 + SUB])[0:1], axis=1, keepdims=True)
+        r_avg = (b2 * r_total + (1.0 - b2) * (s_total / cols_all_out)) / rows_all_out
         root_avg = jnp.sqrt(r_avg)
         cols = col_acc_out[...] + col_peer_out[...]
         c_new_h = b2 * c_out[:, 0:LANE] + (1.0 - b2) * (jnp.sum(cols[0:SUB], axis=0, keepdims=True) / rows_all_out)
@@ -456,8 +427,7 @@
                 acc = acc + sq[SUB * i:SUB * i + SUB]
             return acc
 
-        tot2_out[me] = lax.fori_loop(0, TILES_OUT, body, jnp.zeros((SUB, LANE), F32))
-        to_all(tot2_out, 3)
+        share_squares(lax.fori_loop(0, TILES_OUT, body, jnp.zeros((SUB, LANE), F32)), zt_out, pt_out, ct_out)
 
     def w_load_out():
         first = 5 * (q // QUAD) + j
@@ -467,8 +437,7 @@
         return pltpu.make_async_copy(m_out, m_out_new, load_sem.at[3])
 
     def update_out():
-        from_all(tot2_out, 3)
-        scale = scale_of(tot2_out, float(rows_all_out * cols_all_out))
+        scale = scale_from(ct_out, float(rows_all_out * cols_all_out))
         w_load_out().wait()
         m_load_out().wait()
         bh, bt = vec_x[0:1], vec_y[0:1]
@@ -504,8 +473,11 @@
         lax.fori_loop(0, TILES_OUT, body, 0)
 
     col_acc[...] = jnp.zeros_like(col_acc)
-    start_in(0)
-    start_in(1)
+    own_load(0).start()
+    own_load(1).start()
+    pl.semaphore_wait(barrier, QUAD)
+    pair_in(0).start()
+    pair_in(1).start()
 
     def at_step(cond, fn, *args):
         @pl.when(cond)
@@ -550,16 +522,11 @@
         at_step(within(3 * n, QUAD * n), gather_first, 1, wpk, M_OUT, s - 3 * n)
         at_step(within(3 * n + 2, QUAD * n + 2), gather_second, 1, wpk, M_OUT, s - 3 * n - 2)
         at_step(within(3 * n + QUAD, QUAD * n + QUAD), gather_third, 1, wpk, M_OUT, s - 3 * n - QUAD)
+        at_step(within(2 * n + 6, 3 * n + 6), gather_last, 0, win, M_IN, s - 2 * n - 6)
+        at_step(within(3 * n + 6, QUAD * n + 6), gather_last, 1, wpk, M_OUT, s - 3 * n - 6)
         return 0
 
-    lax.fori_loop(0, QUAD * n + QUAD, step, 0)
-
-    def finish(t, _):
-        gather_last(0, win, M_IN, t)
-        gather_last(1, wpk, M_OUT, t)
-        return 0
-
-    lax.fori_loop(0, n, finish, 0)
+    lax.fori_loop(0, QUAD * n + 6, step, 0)
     pair_out(n - 2).wait_send()
     pair_out(n - 1).wait_send()
 
@@ -651,22 +618,17 @@
             pltpu.VMEM((SUB, COLS_IN), F32),
             pltpu.VMEM((ROWS_IN, LANE), F32),
             pltpu.VMEM((ROWS_IN, LANE), F32),
-            pltpu.VMEM((SUB2, LANE), F32),
-            pltpu.VMEM((SUB2, LANE), F32),
-            pltpu.VMEM((n_dp, 1, COLS_IN), F32),
-            pltpu.VMEM((n_dp, 1, RAW_OUT), F32),
-            pltpu.VMEM((n_tp * n_dp, SUB2, LANE), F32),
-            pltpu.VMEM((n_tp * n_dp, SUB, LANE), F32),
-            pltpu.VMEM((n_tp * n_dp, SUB2, LANE), F32),
-            pltpu.VMEM((n_tp * n_dp, SUB, LANE), F32),
-            dma((2, N_RED, STEPS)),
-            dma((2, N_GAT, STEPS)),
+            pltpu.VMEM((SUB2 + SUB, LANE), F32),
+            pltpu.VMEM((SUB2 + SUB, LANE), F32),
+            pltpu.VMEM((2, 1, COLS_IN + 2 * LANE), F32),
+            pltpu.VMEM((QUAD, 1, COLS_IN + 2 * LANE), F32),
+            pltpu.VMEM((2, 1, RAW_OUT + LANE), F32),
+            pltpu.VMEM((QUAD, 1, RAW_OUT + LANE), F32),
+        ] + [pltpu.VMEM((i, 1, LANE), F32) for i in (2, 2, QUAD)] * 2 + [
+            dma((N_RED, SLOTS)),
+            dma((N_GAT, SLOTS)),
             dma((QUAD,)),
-            dma((2, n_dp)),
-            dma((2, n_dp)),
-            dma((QUAD,)),
-            dma((QUAD, n_tp * n_dp)),
-            dma((QUAD, n_tp * n_dp)),
+            dma((2, 10)),
         ],
         compiler_params=pltpu.CompilerParams(collective_id=0, has_side_effects=True, vmem_limit_bytes=GRANT),
     )

time: 358 us -> 346 us (0.966)
  Pallas kernels: 355 us -> 343 us
    pallas_call x1, Pallas kernels: 341 us -> 329 us  [body(): main(w_in.reshape(shards), w_out[0], g_in.reshape((2, 2, 2, ROWS_IN, COLS...]
where the time goes in v2:
time: 346 us
  Pallas kernels  343 us (99%)
    pallas_call x1, Pallas kernels, body(): main(w_in.reshape(shards), w_out[0], g_in.reshape((2, 2, 2, ROWS_IN, COLS...  329 us
    pallas_call x1, Pallas kernels, body(): final(*[pltpu.with_memory_space_constraint(g, pltpu.VMEM) for g in got])  14.1 us

profile of v2, /device:TPU:0, one launch (start us, length us, event | category | flops | bytes accessed | tf_op | source)
XLA Modules:
  0.0 345.7 jit_solution(11214668995748859212)
XLA Ops:
  2.6 329.1 %shard_map.188 = (f32[4,2,160,4480]{3,2,1,0:T(8,128)S(1)}, f32[4,2,800,640]{3,2,1,0:T(8,128)S(1)}, bf16[160,4480]{1,0:T(8,128)(2,1)S(1)}, bf16[160,3200]{1,0:T(8...) custom-call(f32[4,2,160,4480]{3,2,1,0:T(8,128)} %bitcast.20, ...), custom_call_target="tpu_custom_call" | custom-call | tf_op jit(solution)/shard_map/pallas_call | solution.py:649
  331.7 14.1 %shard_map.189 = (f32[4,2,160,4480]{3,2,1,0:T(8,128)}, f32[3200,1280]{1,0:T(8,128)}, bf16[160,4480]{1,0:T(8,128)(2,1)}, bf16[160,3200]{1,0:T(8,128)(2,1)}, f32[1...) custom-call(f32[4,2,160,4480]{3,2,1,0:T(8,128)S(1)} %get-tuple-element.24.win, ...), custom_call_target="tpu_custom_call" | custom-call | tf_op jit(solution)/shard_map/pallas_call | solution.py:652

commit v3 on v2

--- a/solution.py
+++ b/solution.py
@@ -12,6 +12,7 @@
 MESH = pl.DeviceIdType.MESH
 LANE, SUB, SUB2, PART, QUAD, WIDTH = 128, 8, 16, 32, 4, 160
 NO = None
+BOTH, THREE = pl.ds(0, 2), pl.ds(0, 3)
 
 D = 1280
 ROWS_IN, COLS_IN = WIDTH, 4480
@@ -25,12 +26,13 @@
 
 GRANT = 24 << 20
 
-N_RED = 11
-N_GAT = 16
-SLOTS = 6
-(OWN, DSS, DSR, A1S, A1R, B1S, B1R, A2S, A2R, B2S, B2R) = range(N_RED)
-(OXS, OXR, OYS, OYR, OPS, OPR, FXS, FXR, FYS, FYR, PXS, PXR, PYS, PYR, PDS, PDR) = range(N_GAT)
-
+SLOTS, PAIR_SLOTS = 6, 10
+N_RED, N_GAT, N_EX = 6, 4, 8
+(OWN, DSS, DSR, SENT, R1, R2) = range(N_RED)
+(S1, S2, R_OWN, R_ON) = range(N_GAT)
+(ZS, ZR, CS, CR, TS, TR, BS, BR) = range(N_EX)
+PIECES, PIECE = 5, COLS_IN // 5
+LEN_IN, LEN_OUT = COLS_IN + 3 * LANE, RAW_OUT + LANE
 
 def lanes(shape):
     return lax.broadcasted_iota(jnp.int32, shape, 1)
@@ -49,21 +51,22 @@
 
 
 def main_kernel(n_tp, n_dp, rows_all_in, cols_all_in, rows_all_out, cols_all_out,
-                w_in, w_out, g_in, g_out, m_in, m_out, r_in, c_in, r_out, c_out, lr_ref, wd_ref, b2_ref,
+                w_in, w_out, g_in, g_out, m_in, m_out, r_in_hbm, c_in_hbm, r_out_hbm, c_out_hbm, lr_ref, wd_ref, b2_ref,
                 win, wpk, m_in_new, m_out_new, r_in_new, c_in_new, r_out_new, c_out_new,
                 own_in, raw, packed, gs_in, gs_out, w_cols, ai_out, ai_in, bj_in, vec_x, vec_y,
-                col_acc, row_acc, row_peer, col_acc_out, col_peer_out, v_in, vc_in, v_out, vc_out,
-                zt_in, pt_in, ct_in, zt_out, pt_out, ct_out,
-                red_sem, gat_sem, load_sem, ex_sem):
+                col_acc, row_acc, row_peer, col_acc_out, col_peer_out, v_in, vc_in, vf_in, v_out, vc_out, vf_out,
+                r_in, c_in, r_out, c_out, zt_in, pt_in, ct_in, zt_out, pt_out, ct_out,
+                red_sem, gat_sem, pair_sem, load_sem, ex_sem):
     tp = lax.axis_index('tp')
     q = lax.axis_index('dp')
     p, c = q // 2, q % 2
     y, x = p // 2, p % 2
-    p_x, p_y, p_d = 2 * y + (1 - x), 2 * (1 - y) + x, 2 * (1 - y) + (1 - x)
+    nx, ny, nc = 1 - x, 1 - y, 1 - c
+    p_x, p_y, p_d = 2 * y + nx, 2 * ny + x, 2 * ny + nx
     to_x = {'dp': 2 * p_x + c}
     to_y = {'dp': 2 * p_y + c}
     to_d = {'dp': 2 * p_d + c}
-    to_core = {'dp': 2 * p + (1 - c)}
+    to_core = {'dp': 2 * p + nc}
     to_z = {'tp': 1 - tp}
     j = q % QUAD
     lr, wd, b2 = lr_ref[0], wd_ref[0], b2_ref[0]
@@ -84,19 +87,50 @@
 
     def first_copies(ph, w, m, t):
         _, ra, rb = spans(m, t)
-        a = rcopy(w.at[pl.ds(0, 2), 1 - x, ra], w.at[2, pl.ds(0, 2), ra], red_sem.at[A1S, slot_of(ph, t)], red_sem.at[A1R, slot_of(ph, t)], to_x)
-        b = rcopy(w.at[1 - y, pl.ds(0, 2), rb], w.at[2, pl.ds(0, 2), rb], red_sem.at[B1S, slot_of(ph, t)], red_sem.at[B1R, slot_of(ph, t)], to_y)
+        a = rcopy(w.at[BOTH, nx, ra], w.at[2, BOTH, ra], red_sem.at[SENT, slot_of(ph, t)], red_sem.at[R1, slot_of(ph, t)], to_x)
+        b = rcopy(w.at[ny, BOTH, rb], w.at[2, BOTH, rb], red_sem.at[SENT, slot_of(ph, t)], red_sem.at[R1, slot_of(ph, t)], to_y)
         return a, b
 
     def second_copies(ph, w, m, t):
         _, ra, rb = spans(m, t)
-        a = rcopy(w.at[1 - y, x, ra], w.at[3, 0, ra], red_sem.at[A2S, slot_of(ph, t)], red_sem.at[A2R, slot_of(ph, t)], to_y)
-        b = rcopy(w.at[y, 1 - x, rb], w.at[3, 0, rb], red_sem.at[B2S, slot_of(ph, t)], red_sem.at[B2R, slot_of(ph, t)], to_x)
+        a = rcopy(w.at[ny, x, ra], w.at[3, 0, ra], red_sem.at[SENT, slot_of(ph, t)], red_sem.at[R2, slot_of(ph, t)], to_y)
+        b = rcopy(w.at[y, nx, rb], w.at[3, 0, rb], red_sem.at[SENT, slot_of(ph, t)], red_sem.at[R2, slot_of(ph, t)], to_x)
         return a, b
+
+    def wait_first(ph, w, m, t):
+        rr, _, _ = spans(m, t)
+        part = w.at[2, BOTH, rr]
+        rcopy(part, part, red_sem.at[SENT, slot_of(ph, t)], red_sem.at[R1, slot_of(ph, t)], to_x).wait_recv()
+
+    def wait_second(ph, w, m, t):
+        rr, _, _ = spans(m, t)
+        part = w.at[3, 0, rr]
+        rcopy(part, part, red_sem.at[SENT, slot_of(ph, t)], red_sem.at[R2, slot_of(ph, t)], to_y).wait_recv()
+
+    def wait_sent(ph, w, m, t):
+        rr, _, _ = spans(m, t)
+        part = w.at[THREE, 0, rr]
+        rcopy(part, part, red_sem.at[SENT, slot_of(ph, t)], red_sem.at[R1, slot_of(ph, t)], to_x).wait_send()
 
     def pair_in(t):
         rr, _, _ = spans(M_IN, t)
-        return rcopy(g_in.at[:, :, 1 - c, rr], win.at[pl.ds(0, 2), :, rr], red_sem.at[DSS, slot_of(0, t)], red_sem.at[DSR, slot_of(0, t)], to_core)
+        return rcopy(g_in.at[:, :, nc, rr], win.at[BOTH, :, rr], red_sem.at[DSS, slot_of(0, t)], red_sem.at[DSR, slot_of(0, t)], to_core)
+
+    def piece_in(k):
+        rows, cols = pl.ds(0, 2 * M_IN), pl.ds(PIECE * k, PIECE)
+        return rcopy(g_in.at[:, :, nc, rows, cols], win.at[BOTH, :, rows, cols], red_sem.at[DSS, 0], load_sem.at[2 * QUAD + k], to_core)
+
+    def reduce_start():
+        own_load(0).wait()
+        for k in range(PIECES):
+            cols = pl.ds(PIECE * k, PIECE)
+            piece_in(k).wait_recv()
+            for yy in range(2):
+                for xx in range(2):
+                    win[yy, xx, 0:2 * M_IN, cols] = win[yy, xx, 0:2 * M_IN, cols] + own_in[0, yy, xx, :, cols]
+            ra, rb = pl.ds(0, M_IN), pl.ds(M_IN, M_IN)
+            rcopy(win.at[BOTH, nx, ra, cols], win.at[2, BOTH, ra, cols], red_sem.at[SENT, 0], red_sem.at[R1, 0], to_x).start()
+            rcopy(win.at[ny, BOTH, rb, cols], win.at[2, BOTH, rb, cols], red_sem.at[SENT, 0], red_sem.at[R1, 0], to_y).start()
 
     def own_load(t):
         rr, _, _ = spans(M_IN, t)
@@ -107,7 +141,7 @@
 
     def pair_out(t):
         rr, _, _ = spans(M_OUT, t)
-        return rcopy(packed.at[lax.rem(t, 2), :, :, 1 - c], wpk.at[pl.ds(0, 2), :, rr], red_sem.at[DSS, slot_of(1, t)], red_sem.at[DSR, slot_of(1, t)], to_core)
+        return rcopy(packed.at[lax.rem(t, 2), :, :, nc], wpk.at[BOTH, :, rr], red_sem.at[DSS, slot_of(1, t)], red_sem.at[DSR, slot_of(1, t)], to_core)
 
     def start_in(t):
         own_load(t).start()
@@ -173,28 +207,23 @@
 
     def reduce_second(ph, w, m, t):
         _, ra, rb = spans(m, t)
-        a, b = first_copies(ph, w, m, t)
-        a2, b2_ = second_copies(ph, w, m, t)
+        on_y, on_x = second_copies(ph, w, m, t)
         if ph == 0:
             pair_in(t).wait_send()
-        a.wait_recv()
-        w[1 - y, x, ra] = w[1 - y, x, ra] + w[2, 1 - y, ra]
-        a2.start()
-        b.wait_recv()
-        w[y, 1 - x, rb] = w[y, 1 - x, rb] + w[2, 1 - x, rb]
-        b2_.start()
+        wait_first(ph, w, m, t)
+        w[ny, x, ra] = w[ny, x, ra] + w[2, ny, ra]
+        on_y.start()
+        w[y, nx, rb] = w[y, nx, rb] + w[2, nx, rb]
+        on_x.start()
 
     def reduce_third(ph, w, m, t, gs):
         _, ra, rb = spans(m, t)
-        first, second = first_copies(ph, w, m, t), second_copies(ph, w, m, t)
-        second[0].wait_recv()
+        wait_second(ph, w, m, t)
         ga = w[y, x, ra] + w[2, y, ra] + w[3, 0, ra]
         gs[ra] = ga
-        second[1].wait_recv()
         gb = w[y, x, rb] + w[2, x, rb] + w[3, 0, rb]
         gs[rb] = gb
-        for copy in (*first, *second):
-            copy.wait_send()
+        wait_sent(ph, w, m, t)
         if ph == 0:
             sa, sb = ga * ga + 1e-30, gb * gb + 1e-30
             col_acc[...] = col_acc[...] + (sa + sb)
@@ -204,82 +233,77 @@
                     part = part + sq[:, LANE * i:LANE * i + LANE]
                 row_acc[rows] = part
 
-    def gather_own(ph, w, m, t):
+    def sems(ph, t, send, recv):
+        return gat_sem.at[send, slot_of(ph, t)], gat_sem.at[recv, slot_of(ph, t)]
+
+    def pair_sems(ph, t, send):
+        return gat_sem.at[send, slot_of(ph, t)], pair_sem.at[lax.rem(ph * STEPS + t, PAIR_SLOTS)]
+
+    def gather_first(ph, w, m, t):
         rr, _, _ = spans(m, t)
         src = w.at[p, c, rr]
-        return (rcopy(src, src, gat_sem.at[OXS, slot_of(ph, t)], gat_sem.at[OXR, slot_of(ph, t)], to_x),
-                rcopy(src, src, gat_sem.at[OYS, slot_of(ph, t)], gat_sem.at[OYR, slot_of(ph, t)], to_y),
-                rcopy(src, src, gat_sem.at[OPS, slot_of(ph, t)], gat_sem.at[OPR, slot_of(ph, t)], to_core))
-
-    def gather_came(ph, w, m, t):
+        rcopy(src, src, *sems(ph, t, S1, R_OWN), to_x).start()
+        rcopy(src, src, *sems(ph, t, S1, R_OWN), to_y).start()
+        rcopy(src, src, *pair_sems(ph, t, S1), to_core).start()
+
+    def gather_second(ph, w, m, t):
+        rr, ra, rb = spans(m, t)
+        both = w.at[BOTH, c, rr]
+        rcopy(both, both, *sems(ph, t, S1, R_OWN), to_x).wait_recv()
+        for other, rows, dev in ((p_x, rb, to_y), (p_y, ra, to_x)):
+            rcopy(w.at[other, c, rows], w.at[other, c, rows], *sems(ph, t, S2, R_ON), dev).start()
+            rcopy(w.at[other, c, rr], w.at[other, c, rr], *pair_sems(ph, t, S2), to_core).start()
+
+    def gather_third(ph, w, m, t):
         rr, _, _ = spans(m, t)
-        return (rcopy(w.at[p_x, c, rr], w.at[p_x, c, rr], gat_sem.at[OXS, slot_of(ph, t)], gat_sem.at[OXR, slot_of(ph, t)], to_x),
-                rcopy(w.at[p_y, c, rr], w.at[p_y, c, rr], gat_sem.at[OYS, slot_of(ph, t)], gat_sem.at[OYR, slot_of(ph, t)], to_y))
-
-    def gather_on(ph, w, m, t):
-        _, ra, rb = spans(m, t)
-        return (rcopy(w.at[p_y, c, ra], w.at[p_y, c, ra], gat_sem.at[FXS, slot_of(ph, t)], gat_sem.at[FXR, slot_of(ph, t)], to_x),
-                rcopy(w.at[p_x, c, rb], w.at[p_x, c, rb], gat_sem.at[FYS, slot_of(ph, t)], gat_sem.at[FYR, slot_of(ph, t)], to_y))
-
-    def gather_diag(ph, w, m, t):
-        _, ra, rb = spans(m, t)
-        return (rcopy(w.at[p_d, c, ra], w.at[p_d, c, ra], gat_sem.at[FXS, slot_of(ph, t)], gat_sem.at[FXR, slot_of(ph, t)], to_x),
-                rcopy(w.at[p_d, c, rb], w.at[p_d, c, rb], gat_sem.at[FYS, slot_of(ph, t)], gat_sem.at[FYR, slot_of(ph, t)], to_y))
-
-    def gather_pair(ph, w, m, t, cc):
+        diag = w.at[p_d, c, rr]
+        rcopy(diag, diag, *sems(ph, t, S2, R_ON), to_x).wait_recv()
+        rcopy(diag, diag, *pair_sems(ph, t, S2), to_core).start()
+        three = w.at[THREE, c, rr]
+        rcopy(three, three, *sems(ph, t, S1, R_OWN), to_x).wait_send()
+
+    def gather_last(ph, w, m, t):
         rr, _, _ = spans(m, t)
-        return [rcopy(w.at[pp, cc, rr], w.at[pp, cc, rr], gat_sem.at[s, slot_of(ph, t)], gat_sem.at[s + 1, slot_of(ph, t)], to_core)
-                for pp, s in ((p_x, PXS), (p_y, PYS), (p_d, PDS))]
-
-    def gather_first(ph, w, m, t):
-        for copy in gather_own(ph, w, m, t):
-            copy.start()
-
-    def gather_second(ph, w, m, t):
-        rr, _, _ = spans(m, t)
-        came = gather_came(ph, w, m, t)
-        on = gather_on(ph, w, m, t)
-        pair = gather_pair(ph, w, m, t, c)
-        came[0].wait_recv()
-        on[1].start()
-        pair[0].start()
-        came[1].wait_recv()
-        on[0].start()
-        pair[1].start()
-        rcopy(w.at[p, 1 - c, rr], w.at[p, 1 - c, rr], gat_sem.at[OPS, slot_of(ph, t)], gat_sem.at[OPR, slot_of(ph, t)], to_core).wait_recv()
-
-    def gather_third(ph, w, m, t):
-        diag = gather_diag(ph, w, m, t)
-        diag[0].wait_recv()
-        diag[1].wait_recv()
-        gather_pair(ph, w, m, t, c)[2].start()
-        for copy in gather_pair(ph, w, m, t, 1 - c)[:2]:
-            copy.wait_recv()
-        for copy in gather_own(ph, w, m, t):
-            copy.wait_send()
-
-    def gather_last(ph, w, m, t):
-        gather_pair(ph, w, m, t, 1 - c)[2].wait_recv()
-        for copy in (*gather_on(ph, w, m, t), *gather_pair(ph, w, m, t, c)):
-            copy.wait_send()
+        four = w.at[:, nc, rr]
+        rcopy(four, four, *pair_sems(ph, t, S2), to_core).wait_recv()
+        rcopy(four, four, *pair_sems(ph, t, S2), to_core).wait_send()
 
     def z_share(src, dst, k):
-        return rcopy(src, dst, ex_sem.at[k, 0], ex_sem.at[k, 1], to_z)
+        return rcopy(src, dst, ex_sem.at[k, ZS], ex_sem.at[k, ZR], to_z)
 
     def share(buf, k):
-        copy = rcopy(buf.at[0], buf.at[1], ex_sem.at[k, 2], ex_sem.at[k, 3], to_core)
+        copy = rcopy(buf.at[0], buf.at[1], ex_sem.at[k, CS], ex_sem.at[k, CR], to_core)
         copy.start()
         copy.wait()
         return buf[0] + buf[1]
 
     def to_chips(buf, k):
-        for i, dev in enumerate((to_x, to_y, to_d)):
-            rcopy(buf.at[p], buf.at[p], ex_sem.at[k, QUAD + i], ex_sem.at[k, QUAD + 3 + i], dev).start()
+        for dev in (to_x, to_y, to_d):
+            rcopy(buf.at[p], buf.at[p], ex_sem.at[k, TS], ex_sem.at[k, TR], dev).start()
 
     def from_chips(buf, k):
-        for i, (dev, other) in enumerate(((to_x, p_x), (to_y, p_y), (to_d, p_d))):
-            rcopy(buf.at[other], buf.at[other], ex_sem.at[k, QUAD + i], ex_sem.at[k, QUAD + 3 + i], dev).wait()
+        three = buf.at[THREE]
+        rcopy(three, three, ex_sem.at[k, TS], ex_sem.at[k, TR], to_x).wait()
         return buf[0] + buf[1] + buf[2] + buf[3]
+
+    def halves(length):
+        half = length // 2
+        return pl.ds(aligned(c * half, LANE), half), pl.ds(aligned(nc * half, LANE), half)
+
+    def vector_send(buf, chips, length):
+        mine, other = halves(length)
+        copy = rcopy(buf.at[0, :, other], buf.at[1, :, other], ex_sem.at[0, CS], ex_sem.at[0, CR], to_core)
+        copy.start()
+        copy.wait()
+        chips[p] = buf[0, :, mine] + buf[1, :, mine]
+        to_chips(chips, 0)
+
+    def vector_take(chips, whole, length):
+        mine, _ = halves(length)
+        whole[:, mine] = from_chips(chips, 0)
+        copy = rcopy(whole.at[:, mine], whole.at[:, mine], ex_sem.at[0, BS], ex_sem.at[0, BR], to_core)
+        copy.start()
+        copy.wait()
 
     def old_lanes(ref, width):
         acc = jnp.zeros((1, LANE), F32)
@@ -301,22 +325,29 @@
         mean = jnp.sum(from_chips(ct, 1), axis=1, keepdims=True) / count
         return 0.1 / jnp.maximum(1.0, jnp.sqrt(mean))
 
+    def vec_loads():
+        pairs = ((r_in_hbm, r_in), (c_in_hbm, c_in), (r_out_hbm, r_out), (c_out_hbm, c_out))
+        return [pltpu.make_async_copy(src, dst, load_sem.at[QUAD + i]) for i, (src, dst) in enumerate(pairs)]
+
     def stats_in_send():
+        for load in vec_loads():
+            load.wait()
         copy = z_share(row_acc, row_peer, 0)
         copy.start()
         v_in[0, :, 0:COLS_IN] = jnp.sum(col_acc[...], axis=0, keepdims=True)
         v_in[0, :, COLS_IN + LANE:COLS_IN + 2 * LANE] = old_lanes(r_in, ROWS_IN)
+        v_in[0, :, COLS_IN + 2 * LANE:LEN_IN] = jnp.zeros((1, LANE), F32)
         copy.wait()
         v_in[0, :, COLS_IN:COLS_IN + LANE] = jnp.sum(row_acc[...] + row_peer[...], axis=0, keepdims=True)
-        vc_in[p] = share(v_in, 0)
-        to_chips(vc_in, 0)
+        vector_send(v_in, vc_in, LEN_IN)
         w_load_in().start()
 
     def w_load_in():
         return pltpu.make_async_copy(w_in.at[p, c], win.at[p, c], load_sem.at[0])
 
     def stats_in_norm():
-        vec = from_chips(vc_in, 0)
+        vector_take(vc_in, vf_in, LEN_IN)
+        vec = vf_in[...]
         c_new = b2 * c_in[...] + (1.0 - b2) * (vec[:, 0:COLS_IN] / rows_all_in)
         c_in_new[...] = c_new
         bj_in[...] = 1.0 / jnp.sqrt(c_new)
@@ -397,11 +428,11 @@
         copy.start()
         copy.wait()
         v_out[0, :, RAW_OUT:RAW_OUT + LANE] = jnp.sum(col_acc_out[0:SUB2] + col_peer_out[0:SUB2], axis=0, keepdims=True)
-        vc_out[p] = share(v_out, 0)
-        to_chips(vc_out, 0)
+        vector_send(v_out, vc_out, LEN_OUT)
 
     def stats_out_norm():
-        vec = from_chips(vc_out, 0)
+        vector_take(vc_out, vf_out, LEN_OUT)
+        vec = vf_out[...]
         r_out_new[...] = b2 * r_out[...] + (1.0 - b2) * (vec[:, 0:RAW_OUT] / cols_all_out)
         s_total = jnp.sum(vec[:, RAW_OUT:RAW_OUT + LANE], axis=1, keepdims=True)
         r_total = jnp.sum((col_acc_out[SUB2:SUB2 + SUB] + col_peer_out[SUB2:SUB2 + SUB])[0:1], axis=1, keepdims=True)
@@ -476,8 +507,10 @@
     own_load(0).start()
     own_load(1).start()
     pl.semaphore_wait(barrier, QUAD)
-    pair_in(0).start()
+    for k in range(PIECES):
+        piece_in(k).start()
     pair_in(1).start()
+    reduce_start()
 
     def at_step(cond, fn, *args):
         @pl.when(cond)
@@ -491,12 +524,14 @@
             return jnp.logical_and(s >= lo, s < hi)
 
         at_step(s + 2 < n, start_in, s + 2)
-        at_step(s < n, reduce_first, 0, win, M_IN, s)
+        at_step(within(1, n), reduce_first, 0, win, M_IN, s)
         at_step(within(2, n + 2), reduce_second, 0, win, M_IN, s - 2)
         at_step(within(QUAD, n + QUAD), reduce_third, 0, win, M_IN, s - QUAD, gs_in)
 
         @pl.when(s == 2)
         def _():
+            for copy in vec_loads():
+                copy.start()
             m_load_in().start()
             m_load_out().start()
             w_load_out().start()
@@ -601,7 +636,7 @@
     main = pl.pallas_call(
         functools.partial(main_kernel, n_tp, n_dp, D, COLS_IN * n_tp, RAW_OUT * n_tp, D),
         out_shape=[pltpu.VMEM(shape, dtype) for shape, dtype in kept],
-        in_specs=[hbm] * 6 + [vmem] * QUAD + [smem] * 3,
+        in_specs=[hbm] * 6 + [hbm] * QUAD + [smem] * 3,
         out_specs=[vmem] * SUB,
         scratch_shapes=[
             pltpu.VMEM((3, 2, 2, 2 * M_IN, COLS_IN), F32),
@@ -620,15 +655,22 @@
             pltpu.VMEM((ROWS_IN, LANE), F32),
             pltpu.VMEM((SUB2 + SUB, LANE), F32),
             pltpu.VMEM((SUB2 + SUB, LANE), F32),
-            pltpu.VMEM((2, 1, COLS_IN + 2 * LANE), F32),
-            pltpu.VMEM((QUAD, 1, COLS_IN + 2 * LANE), F32),
-            pltpu.VMEM((2, 1, RAW_OUT + LANE), F32),
-            pltpu.VMEM((QUAD, 1, RAW_OUT + LANE), F32),
+            pltpu.VMEM((2, 1, LEN_IN), F32),
+            pltpu.VMEM((QUAD, 1, LEN_IN // 2), F32),
+            pltpu.VMEM((1, LEN_IN), F32),
+            pltpu.VMEM((2, 1, LEN_OUT), F32),
+            pltpu.VMEM((QUAD, 1, LEN_OUT // 2), F32),
+            pltpu.VMEM((1, LEN_OUT), F32),
+            pltpu.VMEM((1, ROWS_IN), F32),
+            pltpu.VMEM((1, COLS_IN), F32),
+            pltpu.VMEM((1, RAW_OUT), F32),
+            pltpu.VMEM((1, WIDTH), F32),
         ] + [pltpu.VMEM((i, 1, LANE), F32) for i in (2, 2, QUAD)] * 2 + [
             dma((N_RED, SLOTS)),
             dma((N_GAT, SLOTS)),
-            dma((QUAD,)),
-            dma((2, 10)),
+            dma((PAIR_SLOTS,)),
+            dma((2 * QUAD + PIECES,)),
+            dma((2, N_EX)),
         ],
         compiler_params=pltpu.CompilerParams(collective_id=0, has_side_effects=True, vmem_limit_bytes=GRANT),
     )

time: 346 us -> 342 us (0.988)
    pallas_call x1, Pallas kernels: 329 us -> 326 us  [body(): main(w_in.reshape(shards), w_out[0], g_in.reshape((2, 2, 2, ROWS_IN, COLS...]
where the time goes in v3:
time: 342 us
  Pallas kernels  340 us (99%)
    pallas_call x1, Pallas kernels, body(): main(w_in.reshape(shards), w_out[0], g_in.reshape((2, 2, 2, ROWS_IN, COLS...  326 us
    pallas_call x1, Pallas kernels, body(): final(*[pltpu.with_memory_space_constraint(g, pltpu.VMEM) for g in got])  14.1 us

profile of v3, /device:TPU:0, one launch (start us, length us, event | category | flops | bytes accessed | tf_op | source)
XLA Modules:
  0.0 342.1 jit_solution(15298697612473070730)
XLA Ops:
  2.6 325.5 %shard_map.188 = (f32[4,2,160,4480]{3,2,1,0:T(8,128)S(1)}, f32[4,2,800,640]{3,2,1,0:T(8,128)S(1)}, bf16[160,4480]{1,0:T(8,128)(2,1)S(1)}, bf16[160,3200]{1,0:T(8...) custom-call(f32[4,2,160,4480]{3,2,1,0:T(8,128)} %bitcast.20, ...), custom_call_target="tpu_custom_call" | custom-call | tf_op jit(solution)/shard_map/pallas_call | solution.py:691
  328.1 14.1 %shard_map.189 = (f32[4,2,160,4480]{3,2,1,0:T(8,128)}, f32[3200,1280]{1,0:T(8,128)}, bf16[160,4480]{1,0:T(8,128)(2,1)}, bf16[160,3200]{1,0:T(8,128)(2,1)}, f32[1...) custom-call(f32[4,2,160,4480]{3,2,1,0:T(8,128)S(1)} %get-tuple-element.24.win, ...), custom_call_target="tpu_custom_call" | custom-call | tf_op jit(solution)/shard_map/pallas_call | solution.py:694

commit v4 on v3

--- a/solution.py
+++ b/solution.py
@@ -31,8 +31,8 @@
 (OWN, DSS, DSR, SENT, R1, R2) = range(N_RED)
 (S1, S2, R_OWN, R_ON) = range(N_GAT)
 (ZS, ZR, CS, CR, TS, TR, BS, BR) = range(N_EX)
-PIECES, PIECE = 5, COLS_IN // 5
-LEN_IN, LEN_OUT = COLS_IN + 3 * LANE, RAW_OUT + LANE
+PIECES, PIECE = 7, COLS_IN // 7
+LEN_IN, LEN_OUT = COLS_IN + LANE, RAW_OUT + LANE
 
 def lanes(shape):
     return lax.broadcasted_iota(jnp.int32, shape, 1)
@@ -55,7 +55,7 @@
                 win, wpk, m_in_new, m_out_new, r_in_new, c_in_new, r_out_new, c_out_new,
                 own_in, raw, packed, gs_in, gs_out, w_cols, ai_out, ai_in, bj_in, vec_x, vec_y,
                 col_acc, row_acc, row_peer, col_acc_out, col_peer_out, v_in, vc_in, vf_in, v_out, vc_out, vf_out,
-                r_in, c_in, r_out, c_out, zt_in, pt_in, ct_in, zt_out, pt_out, ct_out,
+                r_in, c_in, r_out, c_out, zr, zt_in, pt_in, ct_in, zt_out, pt_out, ct_out,
                 red_sem, gat_sem, pair_sem, load_sem, ex_sem):
     tp = lax.axis_index('tp')
     q = lax.axis_index('dp')
@@ -305,13 +305,6 @@
         copy.start()
         copy.wait()
 
-    def old_lanes(ref, width):
-        acc = jnp.zeros((1, LANE), F32)
-        for i in range(0, width, LANE):
-            part = ref[:, i:min(i + LANE, width)]
-            acc = acc + (part if part.shape[1] == LANE else pad_lanes(part))
-        return acc
-
     def share_squares(acc, zt, pt, ct):
         zt[0] = jnp.sum(acc, axis=0, keepdims=True)
         copy = z_share(zt.at[0], zt.at[1], 1)
@@ -335,10 +328,15 @@
         copy = z_share(row_acc, row_peer, 0)
         copy.start()
         v_in[0, :, 0:COLS_IN] = jnp.sum(col_acc[...], axis=0, keepdims=True)
-        v_in[0, :, COLS_IN + LANE:COLS_IN + 2 * LANE] = old_lanes(r_in, ROWS_IN)
-        v_in[0, :, COLS_IN + 2 * LANE:LEN_IN] = jnp.zeros((1, LANE), F32)
-        copy.wait()
-        v_in[0, :, COLS_IN:COLS_IN + LANE] = jnp.sum(row_acc[...] + row_peer[...], axis=0, keepdims=True)
+        copy.wait()
+        row_mean = jnp.sum(row_acc[...] + row_peer[...], axis=1, keepdims=True) / cols_all_in
+        row_mean = jnp.broadcast_to(row_mean, (ROWS_IN, LANE))
+        r_old = jnp.concatenate([row_to_col(r_in[:, 0:LANE]), row_to_col(pad_lanes(r_in[:, LANE:WIDTH]))[0:PART]], axis=0)
+        r_new = b2 * r_old + (1.0 - b2) * row_mean
+        r_in_new[:, 0:LANE] = r_new[0:LANE].T[0:1]
+        r_in_new[:, LANE:WIDTH] = jnp.concatenate([r_new[LANE:WIDTH], jnp.zeros((LANE - PART, LANE), F32)], axis=0).T[0:1, 0:PART]
+        ai_in[...] = r_new
+        v_in[0, :, COLS_IN:LEN_IN] = jnp.sum(r_new, axis=0, keepdims=True)
         vector_send(v_in, vc_in, LEN_IN)
         w_load_in().start()
 
@@ -351,17 +349,8 @@
         c_new = b2 * c_in[...] + (1.0 - b2) * (vec[:, 0:COLS_IN] / rows_all_in)
         c_in_new[...] = c_new
         bj_in[...] = 1.0 / jnp.sqrt(c_new)
-        s_total = jnp.sum(vec[:, COLS_IN:COLS_IN + LANE], axis=1, keepdims=True)
-        r_total = jnp.sum(vec[:, COLS_IN + LANE:COLS_IN + 2 * LANE], axis=1, keepdims=True)
-        r_avg = (b2 * r_total + (1.0 - b2) * (s_total / cols_all_in)) / rows_all_in
-        root_avg = jnp.sqrt(r_avg)
-        row_mean = jnp.sum(row_acc[...] + row_peer[...], axis=1, keepdims=True) / cols_all_in
-        row_mean = jnp.broadcast_to(row_mean, (ROWS_IN, LANE))
-        r_old = jnp.concatenate([row_to_col(r_in[:, 0:LANE]), row_to_col(pad_lanes(r_in[:, LANE:WIDTH]))[0:PART]], axis=0)
-        r_new = b2 * r_old + (1.0 - b2) * row_mean
-        r_in_new[:, 0:LANE] = r_new[0:LANE].T[0:1]
-        r_in_new[:, LANE:WIDTH] = jnp.concatenate([r_new[LANE:WIDTH], jnp.zeros((96, LANE), F32)], axis=0).T[0:1, 0:PART]
-        ai_in[...] = root_avg / jnp.sqrt(r_new)
+        root_avg = jnp.sqrt(vec[:, COLS_IN:COLS_IN + 1] / rows_all_in)
+        ai_in[...] = root_avg / jnp.sqrt(ai_in[...])
 
         def body(i, acc):
             rows = pl.ds(aligned(SUB * i, SUB), SUB)
@@ -423,21 +412,25 @@
         ah, at = lax.fori_loop(0, TILES_OUT, body, (zero, zero))
         col_acc_out[0:SUB] = ah
         col_acc_out[SUB:SUB2] = at
-        col_acc_out[SUB2:SUB2 + SUB] = jnp.broadcast_to(old_lanes(r_out, RAW_OUT), (SUB, LANE))
         copy = z_share(col_acc_out, col_peer_out, 0)
         copy.start()
         copy.wait()
-        v_out[0, :, RAW_OUT:RAW_OUT + LANE] = jnp.sum(col_acc_out[0:SUB2] + col_peer_out[0:SUB2], axis=0, keepdims=True)
+        v_out[0, :, RAW_OUT:LEN_OUT] = jnp.zeros((1, LANE), F32)
         vector_send(v_out, vc_out, LEN_OUT)
 
     def stats_out_norm():
         vector_take(vc_out, vf_out, LEN_OUT)
         vec = vf_out[...]
-        r_out_new[...] = b2 * r_out[...] + (1.0 - b2) * (vec[:, 0:RAW_OUT] / cols_all_out)
-        s_total = jnp.sum(vec[:, RAW_OUT:RAW_OUT + LANE], axis=1, keepdims=True)
-        r_total = jnp.sum((col_acc_out[SUB2:SUB2 + SUB] + col_peer_out[SUB2:SUB2 + SUB])[0:1], axis=1, keepdims=True)
-        r_avg = (b2 * r_total + (1.0 - b2) * (s_total / cols_all_out)) / rows_all_out
-        root_avg = jnp.sqrt(r_avg)
+        r_new = b2 * r_out[...] + (1.0 - b2) * (vec[:, 0:RAW_OUT] / cols_all_out)
+        r_out_new[...] = r_new
+        part = r_new[:, 0:LANE]
+        for i in range(1, TILES_OUT):
+            part = part + r_new[:, LANE * i:LANE * i + LANE]
+        zr[0] = part
+        copy = rcopy(zr.at[0], zr.at[1], ex_sem.at[1, BS], ex_sem.at[1, BR], to_z)
+        copy.start()
+        copy.wait()
+        root_avg = jnp.sqrt(jnp.sum(zr[0] + zr[1], axis=1, keepdims=True) / rows_all_out)
         cols = col_acc_out[...] + col_peer_out[...]
         c_new_h = b2 * c_out[:, 0:LANE] + (1.0 - b2) * (jnp.sum(cols[0:SUB], axis=0, keepdims=True) / rows_all_out)
         c_new_t = b2 * pad_lanes(c_out[:, LANE:WIDTH]) + (1.0 - b2) * (jnp.sum(cols[SUB:SUB2], axis=0, keepdims=True) / rows_all_out)
@@ -567,9 +560,9 @@
 
 
 def final_kernel(win, wpk, mi, mo, ri, ci, ro, co, win_o, wout_o, mi_o, mo_o, ri_o, ci_o, ro_o, co_o, stage, sem, stage_sem):
-    plain = [pltpu.make_async_copy(win, win_o, sem.at[0])]
+    plain = [pltpu.make_async_copy(win.at[i // 2, i % 2], win_o.at[i // 2, i % 2], sem.at[i]) for i in range(SUB)]
     for i, (src, dst) in enumerate(((mi, mi_o), (mo, mo_o), (ri, ri_o), (ci, ci_o), (ro, ro_o), (co, co_o))):
-        plain.append(pltpu.make_async_copy(src, dst, sem.at[i + 1]))
+        plain.append(pltpu.make_async_copy(src, dst, sem.at[SUB + i]))
     for copy in plain:
         copy.start()
 
@@ -653,8 +646,8 @@
             pltpu.VMEM((SUB, COLS_IN), F32),
             pltpu.VMEM((ROWS_IN, LANE), F32),
             pltpu.VMEM((ROWS_IN, LANE), F32),
-            pltpu.VMEM((SUB2 + SUB, LANE), F32),
-            pltpu.VMEM((SUB2 + SUB, LANE), F32),
+            pltpu.VMEM((SUB2, LANE), F32),
+            pltpu.VMEM((SUB2, LANE), F32),
             pltpu.VMEM((2, 1, LEN_IN), F32),
             pltpu.VMEM((QUAD, 1, LEN_IN // 2), F32),
             pltpu.VMEM((1, LEN_IN), F32),
@@ -665,6 +658,7 @@
             pltpu.VMEM((1, COLS_IN), F32),
             pltpu.VMEM((1, RAW_OUT), F32),
             pltpu.VMEM((1, WIDTH), F32),
+            pltpu.VMEM((2, 1, LANE), F32),
         ] + [pltpu.VMEM((i, 1, LANE), F32) for i in (2, 2, QUAD)] * 2 + [
             dma((N_RED, SLOTS)),
             dma((N_GAT, SLOTS)),
@@ -682,7 +676,7 @@
         ] + [jax.ShapeDtypeStruct(shape, dtype) for shape, dtype in kept[2:]],
         in_specs=[vmem] * SUB,
         out_specs=[hbm] * SUB,
-        scratch_shapes=[pltpu.VMEM((RAW_OUT, D), F32), dma((7,)), dma((STEPS,))],
+        scratch_shapes=[pltpu.VMEM((RAW_OUT, D), F32), dma((14,)), dma((STEPS,))],
         compiler_params=pltpu.CompilerParams(vmem_limit_bytes=GRANT),
     )
 

time: 342 us -> 342 us (level)
  no operation moved by 1% of the time
where the time goes in v4:
time: 342 us
  Pallas kernels  339 us (99%)
    pallas_call x1, Pallas kernels, body(): main(w_in.reshape(shards), w_out[0], g_in.reshape((2, 2, 2, ROWS_IN, COLS...  325 us
    pallas_call x1, Pallas kernels, body(): final(*[pltpu.with_memory_space_constraint(g, pltpu.VMEM) for g in got])  13.7 us

profile of v4, /device:TPU:0, one launch (start us, length us, event | category | flops | bytes accessed | tf_op | source)
XLA Modules:
  0.0 341.6 jit_solution(17877218333192504540)
XLA Ops:
  2.6 325.4 %shard_map.188 = (f32[4,2,160,4480]{3,2,1,0:T(8,128)S(1)}, f32[4,2,800,640]{3,2,1,0:T(8,128)S(1)}, bf16[160,4480]{1,0:T(8,128)(2,1)S(1)}, bf16[160,3200]{1,0:T(8...) custom-call(f32[4,2,160,4480]{3,2,1,0:T(8,128)} %bitcast.20, ...), custom_call_target="tpu_custom_call" | custom-call | tf_op jit(solution)/shard_map/pallas_call | solution.py:685
  328.0 13.7 %shard_map.189 = (f32[4,2,160,4480]{3,2,1,0:T(8,128)}, f32[3200,1280]{1,0:T(8,128)}, bf16[160,4480]{1,0:T(8,128)(2,1)}, bf16[160,3200]{1,0:T(8,128)(2,1)}, f32[1...) custom-call(f32[4,2,160,4480]{3,2,1,0:T(8,128)S(1)} %get-tuple-element.24.win, ...), custom_call_target="tpu_custom_call" | custom-call | tf_op jit(solution)/shard_map/pallas_call | solution.py:688

commit v5 on v4

--- a/solution.py
+++ b/solution.py
@@ -27,9 +27,8 @@
 GRANT = 24 << 20
 
 SLOTS, PAIR_SLOTS = 6, 10
-N_RED, N_GAT, N_EX = 6, 4, 8
-(OWN, DSS, DSR, SENT, R1, R2) = range(N_RED)
-(S1, S2, R_OWN, R_ON) = range(N_GAT)
+N_RED, N_EX = 7, 8
+(OWN, DSS, DSR, SENT, R1, R2, ON) = range(N_RED)
 (ZS, ZR, CS, CR, TS, TR, BS, BR) = range(N_EX)
 PIECES, PIECE = 7, COLS_IN // 7
 LEN_IN, LEN_OUT = COLS_IN + LANE, RAW_OUT + LANE
@@ -56,7 +55,7 @@
                 own_in, raw, packed, gs_in, gs_out, w_cols, ai_out, ai_in, bj_in, vec_x, vec_y,
                 col_acc, row_acc, row_peer, col_acc_out, col_peer_out, v_in, vc_in, vf_in, v_out, vc_out, vf_out,
                 r_in, c_in, r_out, c_out, zr, zt_in, pt_in, ct_in, zt_out, pt_out, ct_out,
-                red_sem, gat_sem, pair_sem, load_sem, ex_sem):
+                red_sem, pair_sem, load_sem, ex_sem):
     tp = lax.axis_index('tp')
     q = lax.axis_index('dp')
     p, c = q // 2, q % 2
@@ -118,7 +117,7 @@
 
     def piece_in(k):
         rows, cols = pl.ds(0, 2 * M_IN), pl.ds(PIECE * k, PIECE)
-        return rcopy(g_in.at[:, :, nc, rows, cols], win.at[BOTH, :, rows, cols], red_sem.at[DSS, 0], load_sem.at[2 * QUAD + k], to_core)
+        return rcopy(g_in.at[:, :, nc, rows, cols], win.at[BOTH, :, rows, cols], red_sem.at[DSS, 0], load_sem.at[k], to_core)
 
     def reduce_start():
         own_load(0).wait()
@@ -234,39 +233,39 @@
                 row_acc[rows] = part
 
     def sems(ph, t, send, recv):
-        return gat_sem.at[send, slot_of(ph, t)], gat_sem.at[recv, slot_of(ph, t)]
+        return red_sem.at[send, slot_of(2 + ph, t)], red_sem.at[recv, slot_of(2 + ph, t)]
 
     def pair_sems(ph, t, send):
-        return gat_sem.at[send, slot_of(ph, t)], pair_sem.at[lax.rem(ph * STEPS + t, PAIR_SLOTS)]
+        return red_sem.at[send, slot_of(2 + ph, t)], pair_sem.at[lax.rem(ph * STEPS + t, PAIR_SLOTS)]
 
     def gather_first(ph, w, m, t):
         rr, _, _ = spans(m, t)
         src = w.at[p, c, rr]
-        rcopy(src, src, *sems(ph, t, S1, R_OWN), to_x).start()
-        rcopy(src, src, *sems(ph, t, S1, R_OWN), to_y).start()
-        rcopy(src, src, *pair_sems(ph, t, S1), to_core).start()
+        rcopy(src, src, *sems(ph, t, SENT, R1), to_x).start()
+        rcopy(src, src, *sems(ph, t, SENT, R1), to_y).start()
+        rcopy(src, src, *pair_sems(ph, t, SENT), to_core).start()
 
     def gather_second(ph, w, m, t):
         rr, ra, rb = spans(m, t)
         both = w.at[BOTH, c, rr]
-        rcopy(both, both, *sems(ph, t, S1, R_OWN), to_x).wait_recv()
+        rcopy(both, both, *sems(ph, t, SENT, R1), to_x).wait_recv()
         for other, rows, dev in ((p_x, rb, to_y), (p_y, ra, to_x)):
-            rcopy(w.at[other, c, rows], w.at[other, c, rows], *sems(ph, t, S2, R_ON), dev).start()
-            rcopy(w.at[other, c, rr], w.at[other, c, rr], *pair_sems(ph, t, S2), to_core).start()
+            rcopy(w.at[other, c, rows], w.at[other, c, rows], *sems(ph, t, ON, R2), dev).start()
+            rcopy(w.at[other, c, rr], w.at[other, c, rr], *pair_sems(ph, t, ON), to_core).start()
 
     def gather_third(ph, w, m, t):
         rr, _, _ = spans(m, t)
         diag = w.at[p_d, c, rr]
-        rcopy(diag, diag, *sems(ph, t, S2, R_ON), to_x).wait_recv()
-        rcopy(diag, diag, *pair_sems(ph, t, S2), to_core).start()
+        rcopy(diag, diag, *sems(ph, t, ON, R2), to_x).wait_recv()
+        rcopy(diag, diag, *pair_sems(ph, t, ON), to_core).start()
         three = w.at[THREE, c, rr]
-        rcopy(three, three, *sems(ph, t, S1, R_OWN), to_x).wait_send()
+        rcopy(three, three, *sems(ph, t, SENT, R1), to_x).wait_send()
 
     def gather_last(ph, w, m, t):
         rr, _, _ = spans(m, t)
         four = w.at[:, nc, rr]
-        rcopy(four, four, *pair_sems(ph, t, S2), to_core).wait_recv()
-        rcopy(four, four, *pair_sems(ph, t, S2), to_core).wait_send()
+        rcopy(four, four, *pair_sems(ph, t, ON), to_core).wait_recv()
+        rcopy(four, four, *pair_sems(ph, t, ON), to_core).wait_send()
 
     def z_share(src, dst, k):
         return rcopy(src, dst, ex_sem.at[k, ZS], ex_sem.at[k, ZR], to_z)
@@ -661,9 +660,8 @@
             pltpu.VMEM((2, 1, LANE), F32),
         ] + [pltpu.VMEM((i, 1, LANE), F32) for i in (2, 2, QUAD)] * 2 + [
             dma((N_RED, SLOTS)),
-            dma((N_GAT, SLOTS)),
             dma((PAIR_SLOTS,)),
-            dma((2 * QUAD + PIECES,)),
+            dma((2 * QUAD,)),
             dma((2, N_EX)),
         ],
         compiler_params=pltpu.CompilerParams(collective_id=0, has_side_effects=True, vmem_limit_bytes=GRANT),

time: 342 us -> 342 us (level)
  no operation moved by 1% of the time
where the time goes in v5:
time: 342 us; the launch traced here: 341 us
  Pallas kernels  339 us (99%)
    pallas_call x1, Pallas kernels, body(): main(w_in.reshape(shards), w_out[0], g_in.reshape((2, 2, 2, ROWS_IN, COLS...  325 us
    pallas_call x1, Pallas kernels, body(): final(*[pltpu.with_memory_space_constraint(g, pltpu.VMEM) for g in got])  13.7 us

profile of v5, /device:TPU:0, one launch (start us, length us, event | category | flops | bytes accessed | tf_op | source)
XLA Modules:
  0.0 341.4 jit_solution(1436292018179751331)
XLA Ops:
  2.6 325.2 %shard_map.188 = (f32[4,2,160,4480]{3,2,1,0:T(8,128)S(1)}, f32[4,2,800,640]{3,2,1,0:T(8,128)S(1)}, bf16[160,4480]{1,0:T(8,128)(2,1)S(1)}, bf16[160,3200]{1,0:T(8...) custom-call(f32[4,2,160,4480]{3,2,1,0:T(8,128)} %bitcast.20, ...), custom_call_target="tpu_custom_call" | custom-call | tf_op jit(solution)/shard_map/pallas_call | solution.py:683
  327.8 13.7 %shard_map.189 = (f32[4,2,160,4480]{3,2,1,0:T(8,128)}, f32[3200,1280]{1,0:T(8,128)}, bf16[160,4480]{1,0:T(8,128)(2,1)}, bf16[160,3200]{1,0:T(8,128)(2,1)}, f32[1...) custom-call(f32[4,2,160,4480]{3,2,1,0:T(8,128)S(1)} %get-tuple-element.24.win, ...), custom_call_target="tpu_custom_call" | custom-call | tf_op jit(solution)/shard_map/pallas_call | solution.py:686

commit v6 on v5

--- a/solution.py
+++ b/solution.py
@@ -30,7 +30,7 @@
 N_RED, N_EX = 7, 8
 (OWN, DSS, DSR, SENT, R1, R2, ON) = range(N_RED)
 (ZS, ZR, CS, CR, TS, TR, BS, BR) = range(N_EX)
-PIECES, PIECE = 7, COLS_IN // 7
+PIECES = (0, 1, 3, 7, 13, 20, 27, COLS_IN // LANE)
 LEN_IN, LEN_OUT = COLS_IN + LANE, RAW_OUT + LANE
 
 def lanes(shape):
@@ -115,14 +115,17 @@
         rr, _, _ = spans(M_IN, t)
         return rcopy(g_in.at[:, :, nc, rr], win.at[BOTH, :, rr], red_sem.at[DSS, slot_of(0, t)], red_sem.at[DSR, slot_of(0, t)], to_core)
 
+    def piece(k):
+        return pl.ds(LANE * PIECES[k], LANE * (PIECES[k + 1] - PIECES[k]))
+
     def piece_in(k):
-        rows, cols = pl.ds(0, 2 * M_IN), pl.ds(PIECE * k, PIECE)
+        rows, cols = pl.ds(0, 2 * M_IN), piece(k)
         return rcopy(g_in.at[:, :, nc, rows, cols], win.at[BOTH, :, rows, cols], red_sem.at[DSS, 0], load_sem.at[k], to_core)
 
     def reduce_start():
         own_load(0).wait()
-        for k in range(PIECES):
-            cols = pl.ds(PIECE * k, PIECE)
+        for k in range(len(PIECES) - 1):
+            cols = piece(k)
             piece_in(k).wait_recv()
             for yy in range(2):
                 for xx in range(2):
@@ -499,7 +502,7 @@
     own_load(0).start()
     own_load(1).start()
     pl.semaphore_wait(barrier, QUAD)
-    for k in range(PIECES):
+    for k in range(len(PIECES) - 1):
         piece_in(k).start()
     pair_in(1).start()
     reduce_start()
@@ -559,9 +562,15 @@
 
 
 def final_kernel(win, wpk, mi, mo, ri, ci, ro, co, win_o, wout_o, mi_o, mo_o, ri_o, ci_o, ro_o, co_o, stage, sem, stage_sem):
-    plain = [pltpu.make_async_copy(win.at[i // 2, i % 2], win_o.at[i // 2, i % 2], sem.at[i]) for i in range(SUB)]
+    def block(i):
+        at = (i // QUAD, (i // 2) % 2, pl.ds(ROWS_IN // 2 * (i % 2), ROWS_IN // 2))
+        return pltpu.make_async_copy(win.at[at], win_o.at[at], sem.at[6])
+
+    for i in range(SUB2):
+        block(i).start()
+    plain = []
     for i, (src, dst) in enumerate(((mi, mi_o), (mo, mo_o), (ri, ri_o), (ci, ci_o), (ro, ro_o), (co, co_o))):
-        plain.append(pltpu.make_async_copy(src, dst, sem.at[SUB + i]))
+        plain.append(pltpu.make_async_copy(src, dst, sem.at[i]))
     for copy in plain:
         copy.start()
 
@@ -569,7 +578,7 @@
         return pl.ds(aligned(RAW_STEP * t, SUB), RAW_STEP)
 
     def put(t):
-        return pltpu.make_async_copy(stage.at[rows_of(t)], wout_o.at[rows_of(t)], stage_sem.at[t])
+        return pltpu.make_async_copy(stage.at[rows_of(t)], wout_o.at[rows_of(t)], stage_sem)
 
     def chunk(t, _):
         def unit(u, _):
@@ -602,8 +611,8 @@
         return 0
 
     lax.fori_loop(0, STEPS, chunk, 0)
-    for t in range(STEPS):
-        put(t).wait()
+    pltpu.make_async_copy(stage, wout_o, stage_sem).wait()
+    pltpu.make_async_copy(win, win_o, sem.at[6]).wait()
     for copy in plain:
         copy.wait()
 
@@ -674,7 +683,7 @@
         ] + [jax.ShapeDtypeStruct(shape, dtype) for shape, dtype in kept[2:]],
         in_specs=[vmem] * SUB,
         out_specs=[hbm] * SUB,
-        scratch_shapes=[pltpu.VMEM((RAW_OUT, D), F32), dma((14,)), dma((STEPS,))],
+        scratch_shapes=[pltpu.VMEM((RAW_OUT, D), F32), dma((7,)), dma],
         compiler_params=pltpu.CompilerParams(vmem_limit_bytes=GRANT),
     )
 

time: 342 us -> 341 us (level)
  no operation moved by 1% of the time
where the time goes in v6:
time: 341 us
  Pallas kernels  338 us (99%)
    pallas_call x1, Pallas kernels, body(): main(w_in.reshape(shards), w_out[0], g_in.reshape((2, 2, 2, ROWS_IN, COLS...  325 us
    pallas_call x1, Pallas kernels, body(): final(*[pltpu.with_memory_space_constraint(g, pltpu.VMEM) for g in got])  13.5 us

profile of v6, /device:TPU:0, one launch (start us, length us, event | category | flops | bytes accessed | tf_op | source)
XLA Modules:
  0.0 341.0 jit_solution(17548891782590263081)
XLA Ops:
  2.6 325.0 %shard_map.188 = (f32[4,2,160,4480]{3,2,1,0:T(8,128)S(1)}, f32[4,2,800,640]{3,2,1,0:T(8,128)S(1)}, bf16[160,4480]{1,0:T(8,128)(2,1)S(1)}, bf16[160,3200]{1,0:T(8...) custom-call(f32[4,2,160,4480]{3,2,1,0:T(8,128)} %bitcast.20, ...), custom_call_target="tpu_custom_call" | custom-call | tf_op jit(solution)/shard_map/pallas_call | solution.py:692
  327.6 13.5 %shard_map.189 = (f32[4,2,160,4480]{3,2,1,0:T(8,128)}, f32[3200,1280]{1,0:T(8,128)}, bf16[160,4480]{1,0:T(8,128)(2,1)}, bf16[160,3200]{1,0:T(8,128)(2,1)}, f32[1...) custom-call(f32[4,2,160,4480]{3,2,1,0:T(8,128)S(1)} %get-tuple-element.24.win, ...), custom_call_target="tpu_custom_call" | custom-call | tf_op jit(solution)/shard_map/pallas_call | solution.py:695

commit v7 on v6

--- a/solution.py
+++ b/solution.py
@@ -27,8 +27,9 @@
 GRANT = 24 << 20
 
 SLOTS, PAIR_SLOTS = 6, 10
-N_RED, N_EX = 7, 8
-(OWN, DSS, DSR, SENT, R1, R2, ON) = range(N_RED)
+N_RED, N_EX = 6, 8
+(OWN, DSS, DSR, SENT, R1, R2) = range(N_RED)
+ON = DSS
 (ZS, ZR, CS, CR, TS, TR, BS, BR) = range(N_EX)
 PIECES = (0, 1, 3, 7, 13, 20, 27, COLS_IN // LANE)
 LEN_IN, LEN_OUT = COLS_IN + LANE, RAW_OUT + LANE
@@ -540,6 +541,7 @@
         at_step(within(n - 1, 2 * n - 1), pack_out, s - n + 1)
         at_step(within(n + 2, 2 * n + 2), reduce_second, 1, wpk, M_OUT, s - n - 2)
         at_step(within(n + QUAD, 2 * n + QUAD), reduce_third, 1, wpk, M_OUT, s - n - QUAD, gs_out)
+        at_step(within(2 * n, 2 * n + 2), lambda t: pair_out(t).wait_send(), s - n - 2)
         at_step(s == n + 3, stats_in_send)
         at_step(s == n + 6, stats_in_norm)
         at_step(s == n + 9, update_in)
@@ -557,8 +559,6 @@
         return 0
 
     lax.fori_loop(0, QUAD * n + 6, step, 0)
-    pair_out(n - 2).wait_send()
-    pair_out(n - 1).wait_send()
 
 
 def final_kernel(win, wpk, mi, mo, ri, ci, ro, co, win_o, wout_o, mi_o, mo_o, ri_o, ci_o, ro_o, co_o, stage, sem, stage_sem):

time: 341 us -> 341 us (level)
  no operation moved by 1% of the time
where the time goes in v7:
time: 341 us
  Pallas kernels  338 us (99%)
    pallas_call x1, Pallas kernels, body(): main(w_in.reshape(shards), w_out[0], g_in.reshape((2, 2, 2, ROWS_IN, COLS...  325 us
    pallas_call x1, Pallas kernels, body(): final(*[pltpu.with_memory_space_constraint(g, pltpu.VMEM) for g in got])  13.5 us

profile of v7, /device:TPU:0, one launch (start us, length us, event | category | flops | bytes accessed | tf_op | source)
XLA Modules:
  0.0 341.0 jit_solution(15184622280951718377)
XLA Ops:
  2.6 324.9 %shard_map.188 = (f32[4,2,160,4480]{3,2,1,0:T(8,128)S(1)}, f32[4,2,800,640]{3,2,1,0:T(8,128)S(1)}, bf16[160,4480]{1,0:T(8,128)(2,1)S(1)}, bf16[160,3200]{1,0:T(8...) custom-call(f32[4,2,160,4480]{3,2,1,0:T(8,128)} %bitcast.20, ...), custom_call_target="tpu_custom_call" | custom-call | tf_op jit(solution)/shard_map/pallas_call | solution.py:692
  327.5 13.5 %shard_map.189 = (f32[4,2,160,4480]{3,2,1,0:T(8,128)}, f32[3200,1280]{1,0:T(8,128)}, bf16[160,4480]{1,0:T(8,128)(2,1)}, bf16[160,3200]{1,0:T(8,128)(2,1)}, f32[1...) custom-call(f32[4,2,160,4480]{3,2,1,0:T(8,128)S(1)} %get-tuple-element.24.win, ...), custom_call_target="tpu_custom_call" | custom-call | tf_op jit(solution)/shard_map/pallas_call | solution.py:695
